TPU v7x, 128 devices: a whole 4x4x4 slice. The times are simulated.
128 devices in a mesh: data: 128 (over z, y, x, core).
Axes of the slice: x: 4, y: 4, z: 4, core: 2. Of those that a mesh axis runs over, the one named last changes fastest.
Arguments:
- z_one: bfloat16 [32768, 128], P('data')
- z_two: bfloat16 [32768, 128], P('data')
- z_small: bfloat16 [4, 32768, 128], P(None, 'data')
- protos: bfloat16 [3000, 128], replicated
- live_mask: int32 [32768], P('data')
Outputs:
- output 1: float32 [32768, 3000], P('data')
- output 2: float32 [32768, 3000], P('data')
- output 3: float32 [], replicated
- output 4: float32 [32768, 128], P('data')
- output 5: float32 [32768, 128], P('data')
- output 6: float32 [4, 32768, 128], P(None, 'data')
- output 7: float32 [3000, 128], replicated
All inputs are finite; a program needn't handle non-finite values.
Results may differ from a plain program's by a relative error of at most 0.001.
Values are sent between devices in bfloat16 or wider.
A program may use at most 1 GiB of HBM per device.

v0:
```python
import jax
import jax.numpy as jnp
from jax import lax
from jax.sharding import PartitionSpec as P

EPS = 0.05
TAU = 0.1
ITERS = 3


def value_a14(scores, live_col, live_total, num_protos):
    weights = live_col * jnp.exp(scores / EPS)
    for step_idx in range(ITERS):
        col_sum = lax.psum(jnp.sum(weights, axis=0), "data")
        weights = weights / (num_protos * col_sum)
        row_sum = jnp.sum(weights, axis=1, keepdims=True)
        row_safe = jnp.where(live_col > 0, row_sum, 1.0)
        weights = weights * (live_col / (live_total * row_safe))
    return live_total * weights


def loss_and_grads(z_one, z_two, z_small, protos, scores_one, scores_two, q_one, q_two, live_col, live_total):
    pair_count = 2 + 2 * z_small.shape[0]
    grad_scale = 1.0 / (TAU * live_total * pair_count)
    scores_small = jnp.einsum("jnd,kd->jnk", z_small, protos, preferred_element_type=jnp.float32)
    logp_one = jax.nn.log_softmax(scores_one / TAU, axis=-1)
    logp_two = jax.nn.log_softmax(scores_two / TAU, axis=-1)
    logp_small = jax.nn.log_softmax(scores_small / TAU, axis=-1)
    q_sum = q_one + q_two
    cross_sum = jnp.sum(q_two * logp_one) + jnp.sum(q_one * logp_two) + jnp.sum(q_sum[None] * logp_small)
    loss_total = -lax.psum(cross_sum, "data") / (live_total * pair_count)
    grad_one = ((live_col * jnp.exp(logp_one) - q_two) * grad_scale).astype(jnp.bfloat16)
    grad_two = ((live_col * jnp.exp(logp_two) - q_one) * grad_scale).astype(jnp.bfloat16)
    grad_small = ((2.0 * live_col[None] * jnp.exp(logp_small) - q_sum[None]) * grad_scale).astype(jnp.bfloat16)
    dz_one = jnp.einsum("nk,kd->nd", grad_one, protos, preferred_element_type=jnp.float32)
    dz_two = jnp.einsum("nk,kd->nd", grad_two, protos, preferred_element_type=jnp.float32)
    dz_small = jnp.einsum("jnk,kd->jnd", grad_small, protos, preferred_element_type=jnp.float32)
    dc_part = (jnp.einsum("nk,nd->kd", grad_one, z_one, preferred_element_type=jnp.float32)
               + jnp.einsum("nk,nd->kd", grad_two, z_two, preferred_element_type=jnp.float32)
               + jnp.einsum("jnk,jnd->kd", grad_small, z_small, preferred_element_type=jnp.float32))
    d_protos = lax.psum(dc_part, "data")
    return loss_total, dz_one, dz_two, dz_small, d_protos


def local_step(z_one, z_two, z_small, protos, live_mask):
    live_f = live_mask.astype(jnp.float32)
    live_col = live_f[:, None]
    live_total = lax.psum(jnp.sum(live_f), "data")
    num_protos = protos.shape[0]
    scores_one = jnp.einsum("nd,kd->nk", z_one, protos, preferred_element_type=jnp.float32)
    q_one = value_a14(scores_one, live_col, live_total, num_protos)
    scores_two = jnp.einsum("nd,kd->nk", z_two, protos, preferred_element_type=jnp.float32)
    q_two = value_a14(scores_two, live_col, live_total, num_protos)
    loss_total, dz_one, dz_two, dz_small, d_protos = loss_and_grads(z_one, z_two, z_small, protos, scores_one, scores_two, q_one, q_two, live_col, live_total)
    return q_one, q_two, loss_total, dz_one, dz_two, dz_small, d_protos


def solution(mesh):
    row_spec = P("data", None)
    crop_spec = P(None, "data", None)
    return jax.shard_map(local_step, mesh=mesh,
                         in_specs=(row_spec, row_spec, crop_spec, P(None, None), P("data")),
                         out_specs=(row_spec, row_spec, P(), row_spec, row_spec, crop_spec, P(None, None)),
                         check_vma=False)
```

profile of v0, /device:TPU:1, one launch (start us, length us, event | category | flops | bytes accessed | tf_op | source)
XLA Modules:
  0.0 626.6 jit_solution(6792652947724246031)
XLA Ops:
  13.6 69.0 %all-reduce = (f32[3000]{0:T(1024)S(1)}, f32[]{:T(128)}) all-reduce(f32[3000]{0:T(1024)S(1)} %get-tuple-element.11, f32[]{:T(128)} %get-tuple-element.29), channel_id=1, replica_groups=mesh['data'=128] {'data'}, use_global_device_ids=true, to_apply=%region_3.0 | all-reduce | flops 3001 | bytes 24008 | tf_op jit(solution)/shard_map/psum | solution.py:14
  82.6 3.9 fusion.40
  90.2 62.9 %psum.65 = f32[3000]{0:T(1024)S(1)} all-reduce(f32[3000]{0:T(1024)S(1)} %multiply_reduce_fusion.9), channel_id=1, replica_groups=mesh['data'=128] {'data'}, use_global_device_ids=true, to_apply=%region_6.7 | all-reduce | flops 3000 | bytes 24000 | tf_op jit(solution)/shard_map/psum | solution.py:14
  153.1 2.4 fusion.39
  157.6 64.2 %psum.66 = f32[3000]{0:T(1024)S(1)} all-reduce(f32[3000]{0:T(1024)S(1)} %multiply_reduce_fusion.8), channel_id=1, replica_groups=mesh['data'=128] {'data'}, use_global_device_ids=true, to_apply=%region_9.10 | all-reduce | flops 3000 | bytes 24000 | tf_op jit(solution)/shard_map/psum | solution.py:14
  221.8 2.4 fusion.25
  227.1 2.4 multiply_convert_fusion.1
  231.3 62.8 %psum.67 = f32[3000]{0:T(1024)S(1)} all-reduce(f32[3000]{0:T(1024)S(1)} %get-tuple-element.9), channel_id=1, replica_groups=mesh['data'=128] {'data'}, use_global_device_ids=true, to_apply=%region_12.13 | all-reduce | flops 3000 | bytes 24000 | tf_op jit(solution)/shard_map/psum | solution.py:14
  294.2 2.8 fusion.37
  299.1 64.4 %psum.68 = f32[3000]{0:T(1024)S(1)} all-reduce(f32[3000]{0:T(1024)S(1)} %multiply_reduce_fusion.7), channel_id=1, replica_groups=mesh['data'=128] {'data'}, use_global_device_ids=true, to_apply=%region_15.16 | all-reduce | flops 3000 | bytes 24000 | tf_op jit(solution)/shard_map/psum | solution.py:14
  363.5 2.4 fusion.36
  367.9 62.7 %psum.69 = f32[3000]{0:T(1024)S(1)} all-reduce(f32[3000]{0:T(1024)S(1)} %multiply_reduce_fusion.6), channel_id=1, replica_groups=mesh['data'=128] {'data'}, use_global_device_ids=true, to_apply=%region_18.19 | all-reduce | flops 3000 | bytes 24000 | tf_op jit(solution)/shard_map/psum | solution.py:14
  430.6 2.5 fusion.26
  433.8 4.1 multiply_convert_fusion.2
  438.0 3.6 fusion.42
  443.3 7.9 %multiply_subtract_fusion = f32[4,256,3000]{1,2,0:T(8,128)} fusion(bf16[4,256,128]{2,1,0:T(8,128)(2,1)S(1)} %copy-done.14, bf16[3000,128]{1,0:T(8,128)(2,1)S(1)} %copy-done), kind=kOutput, calls=%fused_computation.8 | convolution fusion | flops 792580032 | bytes 13318144 | tf_op jit(solution)/shard_map/jit(log_softmax)/sub | solution.py:28
  451.2 13.9 %convolution_bitcast_fusion = f32[3000,128]{1,0:T(8,128)} fusion(bf16[4,256,128]{2,1,0:T(8,128)(2,1)S(1)} %copy-done.14, f32[]{:T(128)S(6)} %div.121, f32[256]{0:T(256)S(1)} %get-tuple-element.28, f32[256,3000]{0,1:T(8,128)} %get-tuple-element.26, f32[4,256,3000]{1,2,0:T(8,128)} %multiply_subtract_fusion), kind=kOutput, calls=%fused_computation.13 | convolution fusion | flops 801796032 | bytes 17159172 | tf_op jit(solution)/shard_map/jnk,jnd->kd/dot_general | solution.py:40
  465.1 3.6 fusion.9
  468.7 13.1 %multiply_reduce_fusion = f32[]{:T(128)} fusion(f32[256,3000]{0,1:T(8,128)} %get-tuple-element.26, f32[4,256,3000]{1,2,0:T(8,128)} %multiply_subtract_fusion), kind=kOutput, calls=%fused_computation.4 | output fusion | flops 9220022 | bytes 15360004 | tf_op jit(solution)/shard_map/jit(log_softmax)/reduce_sum | solution.py:28
  484.4 64.1 %psum.70 = f32[]{:T(128)} all-reduce(f32[]{:T(128)S(6)} %add.35), channel_id=1, replica_groups=mesh['data'=128] {'data'}, use_global_device_ids=true, to_apply=%region_27.29 | all-reduce | flops 1 | bytes 8 | tf_op jit(solution)/shard_map/psum | solution.py:31
  549.1 12.5 %fusion.19 = f32[4,256,128]{2,1,0:T(8,128)} fusion(bf16[3000,128]{1,0:T(8,128)(2,1)S(1)} %copy-done, f32[]{:T(128)S(6)} %div.121, f32[256]{0:T(256)S(1)} %get-tuple-element.28, f32[256,3000]{0,1:T(8,128)} %get-tuple-element.26, f32[4,256,3000]{1,2,0:T(8,128)} %multiply_subtract_fusion), kind=kOutput, calls=%fused_computation.42 | convolution fusion | flops 801796032 | bytes 16653316 | tf_op jit(solution)/shard_map/jnk,kd->jnd/dot_general | solution.py:37
  562.8 2.7 fusion.43
  565.5 50.5 %all-reduce.3.cloned.1.call-done = f32[3000,128]{1,0:T(8,128)} async-done(((f32[3000,128]{1,0:T(8,128)}), f32[3000,128]{1,0:T(8,128)}) %all-reduce.3.cloned.1.call-update) | async-done | bytes 1536016 | tf_op jit(solution)/shard_map/psum | solution.py:41
  616.0 2.6 copy.13
  (61 shorter events, 24.1 us)
Async XLA Ops:
  7.2 2.1 copy-start
  7.2 608.8 %all-reduce.3.cloned.1.call-start = ((), (), s32[]{:S(2)}) async-start(), calls=%async_computation | async-start | bytes 3072000 | tf_op jit(solution)/shard_map/psum | solution.py:41
  10.8 1.6 copy-start.1
  82.6 4.6 copy-start.15
  155.4 1.6 copy-start.4
  157.1 67.7 %copy-start.12 = (bf16[256,128]{1,0:T(8,128)(2,1)S(1)}, bf16[256,128]{1,0:T(8,128)(2,1)}, u32[]{:S(2)}) copy-start(bf16[256,128]{1,0:T(8,128)(2,1)} %param.7) | copy-start | bytes 196612
  224.8 2.3 copy-start.5
  225.6 4.0 copy-start.3
  229.5 1.8 copy-start.8
  297.0 1.6 copy-start.7
  365.8 1.6 copy-start.6
  430.6 3.2 copy-start.2
  433.8 4.1 copy-start.9
  437.9 3.7 copy-start.11
  437.9 3.6 copy-start.10
  437.9 3.6 copy-start.13
  441.6 1.7 copy-start.14
Sparse Core Ops, SparseCore 0:
  468.8 147.1 all-reduce.2
where the time goes:
time: 628 us; the launch traced here: 627 us
  blocking collectives  450 us (72%)
  other arithmetic  52.7 us (8%)
  waiting for transfers between devices  50.5 us (8%)
  matrix products  45.7 us (7%)
  between operations  19.4 us (3%)
  local copies, waits for them, and re-layouts  8.13 us (1%)
    psum x6, blocking collectives, value_a14(): col_sum = lax.psum(jnp.sum(weights, axis=0), 'data')  386 us
    psum x1, blocking collectives, loss_and_grads(): loss_total = -lax.psum(cross_sum, 'data') / (live_total * pair_count)  64.1 us
    psum x1, waiting for transfers between devices, loss_and_grads(): d_protos = lax.psum(dc_part, 'data')  50.5 us
    reduce_sum x6, other arithmetic, value_a14(): row_sum = jnp.sum(weights, axis=1, keepdims=True)  16.2 us
    dot_general x1, matrix products, loss_and_grads(): jnp.einsum('jnk,jnd->kd', grad_small, z_small, preferred_element_type=jnp...  13.9 us
    reduce_sum x1, other arithmetic, loss_and_grads(): logp_small = jax.nn.log_softmax(scores_small / TAU, axis=-1)  13.1 us
  transfers between devices with their start and end apart: 1, of which 1 were waited for; matrix products, arithmetic and copies ran while one was open for 5% of the time, Pallas kernels for 0%

commit v1 on v0

v1 whole, which is shorter than its diff:
```python
import functools
import itertools

import jax
import jax.numpy as jnp
from jax import lax
from jax.experimental import pallas as pl
from jax.experimental.pallas import tpu as pltpu
from jax.sharding import PartitionSpec as P

EPS = 0.05
TAU = 0.1
ITERS = 3
LOG2E = 1.4426950408889634
ROWS = 256
NUM_K = 3000
PAD_K = 3072
TILES = PAD_K // 128
FULL = 11
CHUNK = 256
TAIL = NUM_K - FULL * CHUNK
VIEWS = 6

MESH = pl.DeviceIdType.MESH
STRIDE = {"x": 2, "y": 8, "z": 32}


def group_of(me, axes):
    pos = {a: lax.rem(lax.div(me, STRIDE[a]), 4) for a in axes}
    base = me
    own = 0
    for a in axes:
        base = base - pos[a] * STRIDE[a]
        own = own * 4 + pos[a]
    others = []
    for offs in itertools.product(range(4), repeat=len(axes)):
        if any(offs):
            slot, dev = 0, base
            for a, o in zip(axes, offs):
                q = lax.rem(pos[a] + o, 4)
                slot = slot * 4 + q
                dev = dev + q * STRIDE[a]
            others.append((slot, dev))
    return own, others


def enter(devs):
    bar = pltpu.get_barrier_semaphore()
    for d in devs:
        pl.semaphore_signal(bar, inc=1, device_id=(d,), device_id_type=MESH)
    return lambda: pl.semaphore_wait(bar, len(devs))


def codes_kernel(z_ref, c_ref, m_ref, b_ref, rows_ref, live_ref,
                 zx, mcol, e, colsum, b8, dcol, drecv, slots_a, slots_b,
                 zsend, zrecv, asend, arecv, bsend, brecv, fsend, frecv):
    me = lax.axis_index("data")
    core = lax.rem(me, 2)
    mate = me + 1 - 2 * core
    own_a, others_a = group_of(me, "xy")
    own_b, others_b = group_of(me, "z")
    entered = enter([mate] + [d for _, d in others_a] + [d for _, d in others_b])

    mrow = jnp.broadcast_to(m_ref[...].astype(jnp.float32), (128, ROWS))
    mcol[0] = jnp.concatenate([mrow[:, :128].T, mrow[:, 128:].T], axis=0)

    def build(half, z_half):
        mk = mcol[half][:, :1]

        def piece(scores):
            return jnp.exp2(scores * (LOG2E / EPS)) * mk

        def step(i, carry):
            at = pl.multiple_of(i * CHUNK, CHUNK)
            s = lax.dot_general(z_half, c_ref[pl.ds(at, CHUNK), :], (((1,), (1,)), ((), ())),
                                preferred_element_type=jnp.float32)
            v = piece(s)
            e[pl.ds(half * ROWS, ROWS), pl.ds(at, CHUNK)] = v
            part = jnp.sum(v, axis=0, keepdims=True)
            if half:
                colsum[:, pl.ds(at, CHUNK)] += part
            else:
                colsum[:, pl.ds(at, CHUNK)] = part
            return carry

        lax.fori_loop(0, FULL, step, 0)
        s = lax.dot_general(z_half, c_ref[FULL * CHUNK:NUM_K, :], (((1,), (1,)), ((), ())),
                            preferred_element_type=jnp.float32)
        v = piece(s)
        e[half * ROWS:(half + 1) * ROWS, FULL * CHUNK + 128:] = jnp.zeros((ROWS, 128), jnp.float32)
        e[half * ROWS:(half + 1) * ROWS, FULL * CHUNK:NUM_K] = v
        part = jnp.sum(v, axis=0, keepdims=True)
        if half:
            colsum[:, FULL * CHUNK:NUM_K] += part
        else:
            colsum[:, FULL * CHUNK + 128:] = jnp.zeros((1, 128), jnp.float32)
            colsum[:, FULL * CHUNK:NUM_K] = part

    entered()
    give_z = pltpu.make_async_remote_copy(z_ref.at[1 - core], zx, zsend.at[0], zrecv.at[0],
                                          device_id=(mate,), device_id_type=MESH)
    give_m = pltpu.make_async_remote_copy(mcol.at[0], mcol.at[1], zsend.at[1], zrecv.at[1],
                                          device_id=(mate,), device_id_type=MESH)
    give_z.start()
    give_m.start()
    build(0, z_ref[core])
    give_z.wait()
    give_m.wait()
    build(1, zx[...])

    lane = lax.broadcasted_iota(jnp.int32, (1, 128), 1)
    flat = lax.broadcasted_iota(jnp.int32, (TILES, 128), 0) * 128 + lax.broadcasted_iota(jnp.int32, (TILES, 128), 1)
    count = jnp.sum(mcol[0] + mcol[1], axis=0, keepdims=True)

    def lse_of(view):
        z_view = z_ref[view]

        def step(i, acc):
            at = pl.multiple_of(i * CHUNK, CHUNK)
            s = lax.dot_general(z_view, c_ref[pl.ds(at, CHUNK), :], (((1,), (1,)), ((), ())),
                                preferred_element_type=jnp.float32)
            t = jnp.exp2(s * (LOG2E / TAU))
            return acc + t[:, :128] + t[:, 128:]

        acc = lax.fori_loop(0, FULL, step, jnp.zeros((ROWS, 128), jnp.float32))
        s = lax.dot_general(z_view, c_ref[FULL * CHUNK:NUM_K, :], (((1,), (1,)), ((), ())),
                            preferred_element_type=jnp.float32)
        t = jnp.exp2(s * (LOG2E / TAU))
        total = jnp.sum(acc, axis=1, keepdims=True) + jnp.sum(t, axis=1, keepdims=True)
        rows_ref[:, 2 + view:3 + view] = jnp.log(total)

    def exchange(slots, send, recv, it, own, others, work):
        copies = []
        for k, (_, dev) in enumerate(others):
            copies.append(pltpu.make_async_remote_copy(
                slots.at[it, own], slots.at[it, own], send.at[it, k], recv.at[it, own],
                device_id=(dev,), device_id_type=MESH))
            copies[-1].start()
        work()
        for slot, dev in others:
            pltpu.make_async_remote_copy(
                slots.at[it, slot], slots.at[it, slot], send.at[it, 0], recv.at[it, slot],
                device_id=(dev,), device_id_type=MESH).wait_recv()
        total = slots[it, 0]
        for q in range(1, len(others) + 1):
            total = total + slots[it, q]
        return total, copies

    pending = []
    for it in range(ITERS):
        for t in range(TILES):
            row = colsum[:, t * 128:(t + 1) * 128]
            if it == 0 and t == TILES - 1:
                row = jnp.where(lane == NUM_K % 128, count, row)
            slots_a[it, own_a, t:t + 1, :] = row
        total, copies = exchange(slots_a, asend, arecv, it, own_a, others_a, functools.partial(lse_of, 2 * it))
        pending += copies
        slots_b[it, own_b] = total
        total, copies = exchange(slots_b, bsend, brecv, it, own_b, others_b, functools.partial(lse_of, 2 * it + 1))
        pending += copies
        if it == 0:
            live_ref[...] = jnp.broadcast_to(total[TILES - 1:TILES, NUM_K % 128:NUM_K % 128 + 1], (8, 128))
        inside = flat < NUM_K
        bmat = jnp.where(inside, 1.0 / (NUM_K * jnp.where(inside, total, 1.0)), 0.0)
        if it == ITERS - 1:
            b_ref[core] = bmat
            give_b = pltpu.make_async_remote_copy(b_ref.at[core], b_ref.at[core], fsend.at[0], frecv.at[0],
                                                  device_id=(mate,), device_id_type=MESH)
            give_b.start()
        for t in range(TILES):
            b8[:, t * 128:(t + 1) * 128] = jnp.broadcast_to(bmat[t:t + 1, :], (8, 128))
        if it < ITERS - 1:
            colsum[...] = jnp.zeros_like(colsum)

        def block(i, carry):
            r0 = pl.multiple_of(i * 128, 128)
            acc = jnp.zeros((128, 128), jnp.float32)
            for t in range(TILES):
                acc += (e[pl.ds(r0, 128), t * 128:(t + 1) * 128].reshape(16, 8, 128)
                        * b8[:, t * 128:(t + 1) * 128][None]).reshape(128, 128)
            d = jnp.sum(acc, axis=1, keepdims=True)
            a = jnp.where(d > 0, 1.0 / jnp.where(d > 0, d, 1.0), 0.0)
            if it == ITERS - 1:
                dcol[pl.ds(r0, 128), :] = jnp.broadcast_to(a, (128, 128))
            else:
                ab = jnp.broadcast_to(a, (128, 128))
                for t in range(TILES):
                    colsum[:, t * 128:(t + 1) * 128] += jnp.sum(
                        e[pl.ds(r0, 128), t * 128:(t + 1) * 128] * ab, axis=0, keepdims=True)
            return carry

        lax.fori_loop(0, 2 * ROWS // 128, block, 0)

    give_a = pltpu.make_async_remote_copy(dcol.at[pl.ds(ROWS, ROWS)], drecv, fsend.at[1], frecv.at[1],
                                          device_id=(mate,), device_id_type=MESH)
    give_a.start()
    for c in pending:
        c.wait_send()
    give_b.wait_send()
    pltpu.make_async_remote_copy(b_ref.at[1 - core], b_ref.at[1 - core], fsend.at[0], frecv.at[0],
                                 device_id=(mate,), device_id_type=MESH).wait_recv()
    give_a.wait()
    first = core == 0
    own_r = dcol[:ROWS, :1]
    mate_r = drecv[:, :1]
    rows_ref[:, 0:1] = jnp.where(first, own_r, mate_r)
    rows_ref[:, 1:2] = jnp.where(first, mate_r, own_r)


def run_codes(z_all, protos, mask_row):
    vmem = pl.BlockSpec(memory_space=pltpu.VMEM)
    dma = pltpu.SemaphoreType.DMA
    return pl.pallas_call(
        codes_kernel,
        out_shape=(jax.ShapeDtypeStruct((2, TILES, 128), jnp.float32),
                   jax.ShapeDtypeStruct((ROWS, 128), jnp.float32),
                   jax.ShapeDtypeStruct((8, 128), jnp.float32)),
        in_specs=[vmem] * 3,
        out_specs=(vmem,) * 3,
        scratch_shapes=[
            pltpu.VMEM((ROWS, 128), jnp.bfloat16),
            pltpu.VMEM((2, ROWS, 128), jnp.float32),
            pltpu.VMEM((2 * ROWS, PAD_K), jnp.float32),
            pltpu.VMEM((1, PAD_K), jnp.float32),
            pltpu.VMEM((8, PAD_K), jnp.float32),
            pltpu.VMEM((2 * ROWS, 128), jnp.float32),
            pltpu.VMEM((ROWS, 128), jnp.float32),
            pltpu.VMEM((ITERS, 16, TILES, 128), jnp.float32),
            pltpu.VMEM((ITERS, 4, TILES, 128), jnp.float32),
            dma((2,)), dma((2,)),
            dma((ITERS, 15)), dma((ITERS, 16)),
            dma((ITERS, 3)), dma((ITERS, 4)),
            dma((2,)), dma((2,)),
        ],
        name="codes",
        compiler_params=pltpu.CompilerParams(collective_id=0, has_side_effects=True),
    )(z_all, protos, mask_row)


def local_step(z_one, z_two, z_small, protos, live_mask):
    live_col = live_mask.astype(jnp.float32)[:, None]
    z_all = jnp.concatenate([z_one[None], z_two[None], z_small], axis=0)
    bmat, rows, live = run_codes(z_all, protos, live_mask[None, :])
    live_total = live[0, 0]
    pair_count = 2 + 2 * z_small.shape[0]
    grad_scale = 1.0 / (TAU * live_total * pair_count)
    b = bmat.reshape(2, 1, PAD_K)[:, :, :NUM_K]
    scores = jnp.einsum("vnd,kd->vnk", z_all, protos, preferred_element_type=jnp.float32)
    q = jnp.exp(scores[:2] / EPS) * b * rows[:, :2].T[:, :, None]
    logp = scores / TAU - rows[:, 2:8].T[:, :, None]
    q_one, q_two = q[0], q[1]
    q_sum = q_one + q_two
    cross_sum = jnp.sum(q_two * logp[0]) + jnp.sum(q_one * logp[1]) + jnp.sum(q_sum[None] * logp[2:])
    grad_one = ((live_col * jnp.exp(logp[0]) - q_two) * grad_scale).astype(jnp.bfloat16)
    grad_two = ((live_col * jnp.exp(logp[1]) - q_one) * grad_scale).astype(jnp.bfloat16)
    grad_small = ((2.0 * live_col[None] * jnp.exp(logp[2:]) - q_sum[None]) * grad_scale).astype(jnp.bfloat16)
    grads = jnp.concatenate([grad_one[None], grad_two[None], grad_small], axis=0)
    dz = jnp.einsum("jnk,kd->jnd", grads, protos, preferred_element_type=jnp.float32)
    dc_part = jnp.einsum("jnk,jnd->kd", grads, z_all, preferred_element_type=jnp.float32)
    d_protos = lax.psum(dc_part, "data")
    loss_total = -lax.psum(cross_sum, "data") / (live_total * pair_count)
    return q_one, q_two, loss_total, dz[0], dz[1], dz[2:], d_protos


def solution(mesh):
    row_spec = P("data", None)
    crop_spec = P(None, "data", None)
    return jax.shard_map(local_step, mesh=mesh,
                         in_specs=(row_spec, row_spec, crop_spec, P(None, None), P("data")),
                         out_specs=(row_spec, row_spec, P(), row_spec, row_spec, crop_spec, P(None, None)),
                         check_vma=False)
```

time: 628 us -> 264 us (0.42)
  blocking collectives: 450 us -> 63.8 us
  Pallas kernels: 0 us -> 48.2 us
  other arithmetic: 52.7 us -> 26.3 us
  matrix products: 45.7 us -> 24.6 us
  waiting for transfers between devices: 50.5 us -> 65.2 us
  local copies, waits for them, and re-layouts: 8.13 us -> 15.9 us
    psum x7 -> x1, blocking collectives: 450 us -> 63.8 us  [local_step(): loss_total = -lax.psum(cross_sum, 'data') / (live_total * pair_count)]
    pallas_call x0 -> x1, Pallas kernels: none -> 48.2 us  [run_codes(): pl.pallas_call(codes_kernel, out_shape=(jax.ShapeDtypeStruct((2, TILES, 1...]
    reduce_sum x14 -> x1, other arithmetic: 36.6 us -> 8.91 us  [local_step(): jnp.sum(q_one * logp[1])]
    psum x1, waiting for transfers between devices: 50.5 us -> 65.2 us  [local_step(): d_protos = lax.psum(dc_part, 'data')]
    dot_general x8 -> x3, matrix products: 37.8 us -> 24.6 us  [the longest x1 15.7 us: local_step(): jnp.einsum('vnd,kd->vnk', z_all, protos, preferred_element_type=jnp.float32)]
    sub x1 -> x0, matrix products: 7.9 us -> none  [loss_and_grads(): logp_small = jax.nn.log_softmax(scores_small / TAU, axis=-1)]
  transfers between devices with their start and end apart: 1 -> 1, of which waited for: 1 -> 1; matrix products, arithmetic and copies ran while one was open for 5% -> 6% of each run, Pallas kernels for 0% -> 0%
where the time goes in v1:
time: 264 us; the launch traced here: 263 us
  waiting for transfers between devices  65.2 us (25%)
  blocking collectives  63.8 us (24%)
  Pallas kernels  48.2 us (18%)
  other arithmetic  26.3 us (10%)
  matrix products  24.6 us (9%)
  between operations  19.3 us (7%)
  local copies, waits for them, and re-layouts  15.9 us (6%)
    psum x1, waiting for transfers between devices, local_step(): d_protos = lax.psum(dc_part, 'data')  65.2 us
    psum x1, blocking collectives, local_step(): loss_total = -lax.psum(cross_sum, 'data') / (live_total * pair_count)  63.8 us
    pallas_call x1, Pallas kernels, run_codes(): pl.pallas_call(codes_kernel, out_shape=(jax.ShapeDtypeStruct((2, TILES, 1...  48.2 us
    dot_general x1, matrix products, local_step(): jnp.einsum('vnd,kd->vnk', z_all, protos, preferred_element_type=jnp.float32)  15.7 us
    unnamed x17, local copies, waits for them, and re-layouts  10.3 us
    reduce_sum x1, other arithmetic, local_step(): jnp.sum(q_one * logp[1])  8.91 us
    convert_element_type x1, other arithmetic, local_step(): ((live_col * jnp.exp(logp[0]) - q_two) * grad_scale).astype(jnp.bfloat16)  5.81 us
  transfers between devices with their start and end apart: 1, of which 1 were waited for; matrix products, arithmetic and copies ran while one was open for 6% of the time, Pallas kernels for 0%

profile of v1, /device:TPU:1, one launch (start us, length us, event | category | flops | bytes accessed | tf_op | source)
XLA Modules:
  0.0 263.3 jit_solution(5163577922052228633)
XLA Ops:
  7.2 0.7 broadcast_multiply_fusion
  7.9 0.7 convert_element_type.14
  8.6 1.8 pad_maximum_fusion.5.z_ref
  10.3 48.2 %codes.1 = (f32[2,24,128]{2,1,0:T(8,128)}, f32[256,128]{1,0:T(8,128)}, f32[8,128]{1,0:T(8,128)}) custom-call(bf16[6,256,128]{2,1,0:T(8,128)(2,1)} %pad_maximum_fusion.5.z_ref, bf16[3000,128]{1,0:T(8,128)(2,1)} %c_ref.1, s32[1,256]{1,0:T(1,128)} %bitcast.46), custom_call_target="tpu_custom_call" | custom-call | tf_op jit(solution)/shard_map/codes/pallas_call | solution.py:213
  58.5 1.0 slice_bitcast_fusion.4
  59.5 0.9 slice_bitcast_fusion.5
  60.5 1.2 slice.51
  61.6 0.8 reshape.35
  62.4 0.1 copy.13
  62.5 0.1 copy.12
  62.6 15.7 %multiply_subtract_fusion = (f32[6,256,3000]{1,2,0:T(8,128)}, f32[6,256,3000]{1,2,0:T(8,128)}) fusion(f32[6,256]{1,0:T(8,128)S(1)} %copy.13, bf16[3000,128]{1,0:T(8,128)(2,1)} %c_ref.1, bf16[4,256,128]{2,1,0:T(8,128)(2,1)} %param.7, bf16[1,256,128]{2,1,0:T(8,128)(2,1)} %bitcast.41, bf16[1,256,128]{2,1,0:T(8,128)(2,1)} %bitcast.44), kind=kOutput, calls=%fused_computation | convolution fusion | flops 1189257216 | bytes 38031360 | tf_op jit(solution)/shard_map/vnd,kd->vnk/dot_general | solution.py:248
  79.0 4.1 %fusion.2 = f32[2,256,3000]{1,2,0:T(8,128)S(1)} fusion(f32[6,256,3000]{1,2,0:T(8,128)} %get-tuple-element.25, f32[2,256]{1,0:T(2,128)S(1)} %copy.12, f32[2,3000]{1,0:T(2,128)S(1)} %slice_bitcast_fusion.6), kind=kLoop, calls=%fused_computation.7 | loop fusion | flops 4608000 | bytes 12314048 | tf_op jit(solution)/shard_map/mul | solution.py:249
  83.1 5.8 %multiply_convert_fusion.2 = (bf16[1,256,3000]{1,2,0:T(8,128)(2,1)S(1)}, bf16[1,256,3000]{1,2,0:T(8,128)(2,1)S(1)}, f32[256,3000]{0,1:T(8,128)S(1)}) fusion(f32[6,256,3000]{1,2,0:T(8,128)} %get-tuple-element.24, f32[2,256,3000]{1,2,0:T(8,128)S(1)} %fusion.2, f32[]{:T(128)} %bitcast.13, f32[256]{0:T(256)S(1)} %convert_element_type.14), kind=kLoop, calls=%fused_computation.16 | loop fusion | flops 6912000 | bytes 18433028 | tf_op jit(solution)/shard_map/convert_element_type | solution.py:254
  88.9 5.0 %copy-done = f32[6,256,3000]{1,2,0:T(8,128)S(1)} copy-done((f32[6,256,3000]{1,2,0:T(8,128)S(1)}, f32[6,256,3000]{1,2,0:T(8,128)}, u32[]{:S(2)}) %copy-start) | copy-done | bytes 18432024
  93.9 4.4 %multiply_convert_fusion = (bf16[4,256,3000]{1,2,0:T(8,128)(2,1)S(1)}, f32[]{:T(128)}) fusion(f32[6,256,3000]{1,2,0:T(8,128)S(1)} %copy-done, f32[]{:T(128)} %bitcast.13, f32[256]{0:T(256)S(1)} %broadcast_multiply_fusion, f32[256,3000]{0,1:T(8,128)S(1)} %get-tuple-element.21), kind=kLoop, calls=%fused_computation.1 | loop fusion | flops 18432000 | bytes 21505032 | tf_op jit(solution)/shard_map/convert_element_type | solution.py:256
  98.4 2.7 %copy-done.2 = bf16[4,256,3000]{1,2,0:T(8,128)(2,1)} copy-done((bf16[4,256,3000]{1,2,0:T(8,128)(2,1)}, bf16[4,256,3000]{1,2,0:T(8,128)(2,1)S(1)}, u32[]{:S(2)}) %copy-start.2) | copy-done | bytes 6144024
  101.1 3.9 %fusion.5 = f32[3000,128]{1,0:T(8,128)} fusion(bf16[4,256,3000]{1,2,0:T(8,128)(2,1)S(1)} %get-tuple-element.19, bf16[1,256,3000]{1,2,0:T(8,128)(2,1)S(1)} %get-tuple-element.18, bf16[1,256,3000]{1,2,0:T(8,128)(2,1)S(1)} %get-tuple-element.17, bf16[4,256,128]{2,1,0:T(8,128)(2,1)S(1)} %copy-done.5, bf16[1,256,128]{2,1,0:T(8,128)(2,1)S(1)} %bitcast.42, ...), kind=kOutput, calls=%fused_computation.10 | convolution fusion | flops 1189257216 | bytes 11145216 | tf_op jit(solution)/shard_map/jnk,jnd->kd/dot_general | solution.py:259
  104.9 8.9 %fusion.6 = (f32[]{:T(128)}, f32[]{:T(128)}, f32[256,3000]{0,1:T(8,128)}, f32[256,3000]{0,1:T(8,128)}) fusion(f32[6,256,3000]{1,2,0:T(8,128)} %get-tuple-element.24, f32[2,256,3000]{1,2,0:T(8,128)} %copy-done.1), kind=kLoop, calls=%fused_computation.12 | loop fusion | flops 3071998 | bytes 18432008 | tf_op jit(solution)/shard_map/reduce_sum | solution.py:253
  116.4 63.8 %psum.14 = f32[]{:T(128)} all-reduce(f32[]{:T(128)S(6)} %add.16), channel_id=1, replica_groups=mesh['data'=128] {'data'}, use_global_device_ids=true, to_apply=%region_3.0 | all-reduce | flops 1 | bytes 8 | tf_op jit(solution)/shard_map/psum | solution.py:261
  180.9 5.0 %fusion.4 = f32[6,256,128]{2,1,0:T(8,128)S(1)} fusion(bf16[4,256,3000]{1,2,0:T(8,128)(2,1)} %copy-done.2, bf16[1,256,3000]{1,2,0:T(8,128)(2,1)} %copy-done.4, bf16[1,256,3000]{1,2,0:T(8,128)(2,1)S(1)} %get-tuple-element.17, bf16[3000,128]{1,0:T(8,128)(2,1)S(1)} %copy-done.3), kind=kOutput, calls=%fused_computation.9 | convolution fusion | flops 1188864000 | bytes 10770432 | tf_op jit(solution)/shard_map/jnk,kd->jnd/dot_general | solution.py:258
  185.9 0.8 slice.64
  186.8 0.7 slice_bitcast_fusion.2
  187.5 65.2 %all-reduce.2.cloned.1.call-done = f32[3000,128]{1,0:T(8,128)} async-done(((f32[3000,128]{1,0:T(8,128)}), f32[3000,128]{1,0:T(8,128)}) %all-reduce.2.cloned.1.call-update) | async-done | bytes 1536016 | tf_op jit(solution)/shard_map/psum | solution.py:260
  252.7 2.6 copy.15
  (17 shorter events, 0.1 us)
Async XLA Ops:
  7.2 245.5 %all-reduce.2.cloned.1.call-start = ((), (), s32[]{:S(2)}) async-start(), calls=%async_computation | async-start | bytes 3072000 | tf_op jit(solution)/shard_map/psum | solution.py:260
  83.1 5.8 %copy-start.1 = (f32[2,256,3000]{1,2,0:T(8,128)}, f32[2,256,3000]{1,2,0:T(8,128)S(1)}, u32[]{:S(2)}) copy-start(f32[2,256,3000]{1,2,0:T(8,128)S(1)} %fusion.2) | copy-start | bytes 18432004
  83.1 10.8 %copy-start = (f32[6,256,3000]{1,2,0:T(8,128)S(1)}, f32[6,256,3000]{1,2,0:T(8,128)}, u32[]{:S(2)}) copy-start(f32[6,256,3000]{1,2,0:T(8,128)} %get-tuple-element.24) | copy-start | bytes 55296004
  88.9 9.4 %copy-start.4 = (bf16[1,256,3000]{1,2,0:T(8,128)(2,1)}, bf16[1,256,3000]{1,2,0:T(8,128)(2,1)S(1)}, u32[]{:S(2)}) copy-start(bf16[1,256,3000]{1,2,0:T(8,128)(2,1)S(1)} %get-tuple-element.18) | copy-start | bytes 4608004
  93.9 7.1 %copy-start.5 = (bf16[4,256,128]{2,1,0:T(8,128)(2,1)S(1)}, bf16[4,256,128]{2,1,0:T(8,128)(2,1)}, u32[]{:S(2)}) copy-start(bf16[4,256,128]{2,1,0:T(8,128)(2,1)} %param.7) | copy-start | bytes 786436
  93.9 7.1 %copy-start.6 = (bf16[256,128]{1,0:T(8,128)(2,1)S(1)}, bf16[256,128]{1,0:T(8,128)(2,1)}, u32[]{:S(2)}) copy-start(bf16[256,128]{1,0:T(8,128)(2,1)} %param.6) | copy-start | bytes 196612
  93.9 7.1 %copy-start.7 = (bf16[256,128]{1,0:T(8,128)(2,1)S(1)}, bf16[256,128]{1,0:T(8,128)(2,1)}, u32[]{:S(2)}) copy-start(bf16[256,128]{1,0:T(8,128)(2,1)} %param.5) | copy-start | bytes 196612
  98.4 2.7 %copy-start.2 = (bf16[4,256,3000]{1,2,0:T(8,128)(2,1)}, bf16[4,256,3000]{1,2,0:T(8,128)(2,1)S(1)}, u32[]{:S(2)}) copy-start(bf16[4,256,3000]{1,2,0:T(8,128)(2,1)S(1)} %get-tuple-element.19) | copy-start | bytes 18432004
  104.9 76.0 %copy-start.3 = (bf16[3000,128]{1,0:T(8,128)(2,1)S(1)}, bf16[3000,128]{1,0:T(8,128)(2,1)}, u32[]{:S(2)}) copy-start(bf16[3000,128]{1,0:T(8,128)(2,1)} %c_ref.1) | copy-start | bytes 2304004
Sparse Core Ops, SparseCore 0:
  105.0 147.5 all-reduce.1

commit v2 on v1

--- a/solution.py
+++ b/solution.py
@@ -51,8 +51,8 @@
     return lambda: pl.semaphore_wait(bar, len(devs))
 
 
-def codes_kernel(z_ref, c_ref, m_ref, b_ref, rows_ref, live_ref,
-                 zx, mcol, e, colsum, b8, dcol, drecv, slots_a, slots_b,
+def codes_kernel(z1_ref, z2_ref, zs_ref, c_ref, m_ref, b_ref, rows_ref, live_ref,
+                 z_ref, zx, mcol, e, colsum, dcol, drecv, slots_a, slots_b,
                  zsend, zrecv, asend, arecv, bsend, brecv, fsend, frecv):
     me = lax.axis_index("data")
     core = lax.rem(me, 2)
@@ -61,6 +61,8 @@
     own_b, others_b = group_of(me, "z")
     entered = enter([mate] + [d for _, d in others_a] + [d for _, d in others_b])
 
+    z_ref[0] = z1_ref[...]
+    z_ref[1] = z2_ref[...]
     mrow = jnp.broadcast_to(m_ref[...].astype(jnp.float32), (128, ROWS))
     mcol[0] = jnp.concatenate([mrow[:, :128].T, mrow[:, 128:].T], axis=0)
 
@@ -113,7 +115,7 @@
     count = jnp.sum(mcol[0] + mcol[1], axis=0, keepdims=True)
 
     def lse_of(view):
-        z_view = z_ref[view]
+        z_view = z_ref[view] if view < 2 else zs_ref[view - 2]
 
         def step(i, acc):
             at = pl.multiple_of(i * CHUNK, CHUNK)
@@ -127,7 +129,10 @@
                             preferred_element_type=jnp.float32)
         t = jnp.exp2(s * (LOG2E / TAU))
         total = jnp.sum(acc, axis=1, keepdims=True) + jnp.sum(t, axis=1, keepdims=True)
-        rows_ref[:, 2 + view:3 + view] = jnp.log(total)
+        live = mcol[0][:, :1]
+        rows_ref[:, 2 + view:3 + view] = live / total
+        lse = jnp.log(total) * (live if view < 2 else 2.0 * live)
+        rows_ref[:, 8:9] = lse if view == 0 else rows_ref[:, 8:9] + lse
 
     def exchange(slots, send, recv, it, own, others, work):
         copies = []
@@ -162,13 +167,12 @@
             live_ref[...] = jnp.broadcast_to(total[TILES - 1:TILES, NUM_K % 128:NUM_K % 128 + 1], (8, 128))
         inside = flat < NUM_K
         bmat = jnp.where(inside, 1.0 / (NUM_K * jnp.where(inside, total, 1.0)), 0.0)
+        for t in range(TILES):
+            b_ref[core, :, t * 128:(t + 1) * 128] = jnp.broadcast_to(bmat[t:t + 1, :], (8, 128))
         if it == ITERS - 1:
-            b_ref[core] = bmat
             give_b = pltpu.make_async_remote_copy(b_ref.at[core], b_ref.at[core], fsend.at[0], frecv.at[0],
                                                   device_id=(mate,), device_id_type=MESH)
             give_b.start()
-        for t in range(TILES):
-            b8[:, t * 128:(t + 1) * 128] = jnp.broadcast_to(bmat[t:t + 1, :], (8, 128))
         if it < ITERS - 1:
             colsum[...] = jnp.zeros_like(colsum)
 
@@ -177,7 +181,7 @@
             acc = jnp.zeros((128, 128), jnp.float32)
             for t in range(TILES):
                 acc += (e[pl.ds(r0, 128), t * 128:(t + 1) * 128].reshape(16, 8, 128)
-                        * b8[:, t * 128:(t + 1) * 128][None]).reshape(128, 128)
+                        * b_ref[core, :, t * 128:(t + 1) * 128][None]).reshape(128, 128)
             d = jnp.sum(acc, axis=1, keepdims=True)
             a = jnp.where(d > 0, 1.0 / jnp.where(d > 0, d, 1.0), 0.0)
             if it == ITERS - 1:
@@ -207,22 +211,22 @@
     rows_ref[:, 1:2] = jnp.where(first, mate_r, own_r)
 
 
-def run_codes(z_all, protos, mask_row):
+def run_codes(z_one, z_two, z_small, protos, mask_row):
     vmem = pl.BlockSpec(memory_space=pltpu.VMEM)
     dma = pltpu.SemaphoreType.DMA
     return pl.pallas_call(
         codes_kernel,
-        out_shape=(jax.ShapeDtypeStruct((2, TILES, 128), jnp.float32),
+        out_shape=(jax.ShapeDtypeStruct((2, 8, PAD_K), jnp.float32),
                    jax.ShapeDtypeStruct((ROWS, 128), jnp.float32),
                    jax.ShapeDtypeStruct((8, 128), jnp.float32)),
-        in_specs=[vmem] * 3,
+        in_specs=[vmem] * 5,
         out_specs=(vmem,) * 3,
         scratch_shapes=[
+            pltpu.VMEM((2, ROWS, 128), jnp.bfloat16),
             pltpu.VMEM((ROWS, 128), jnp.bfloat16),
             pltpu.VMEM((2, ROWS, 128), jnp.float32),
             pltpu.VMEM((2 * ROWS, PAD_K), jnp.float32),
             pltpu.VMEM((1, PAD_K), jnp.float32),
-            pltpu.VMEM((8, PAD_K), jnp.float32),
             pltpu.VMEM((2 * ROWS, 128), jnp.float32),
             pltpu.VMEM((ROWS, 128), jnp.float32),
             pltpu.VMEM((ITERS, 16, TILES, 128), jnp.float32),
@@ -234,32 +238,219 @@
         ],
         name="codes",
         compiler_params=pltpu.CompilerParams(collective_id=0, has_side_effects=True),
-    )(z_all, protos, mask_row)
+    )(z_one, z_two, z_small, protos, mask_row)
+
+
+KC = 512
+STEPS = PAD_K // KC
+RB = 16
+
+
+def grads_kernel(z1_ref, z2_ref, zs_ref, c_ref, b_ref, rows_ref, live_ref,
+                 q1_ref, q2_ref, dz1_ref, dz2_ref, dzs_ref, dc_ref,
+                 zall, cm, s_all, g_all, dz_acc, loss_acc):
+    i = pl.program_id(0)
+
+    @pl.when(i == 0)
+    def _():
+        zall[0:ROWS] = z1_ref[...]
+        zall[ROWS:2 * ROWS] = z2_ref[...]
+        for j in range(4):
+            zall[(2 + j) * ROWS:(3 + j) * ROWS] = zs_ref[j]
+        dz_acc[...] = jnp.zeros_like(dz_acc)
+        loss_acc[...] = jnp.zeros_like(loss_acc)
+
+    row_id = lax.broadcasted_iota(jnp.int32, (KC, 128), 0) + i * KC
+    cm[...] = jnp.where(row_id < NUM_K, c_ref[...].astype(jnp.float32), 0.0).astype(jnp.bfloat16)
+    s_all[...] = lax.dot_general(zall[...], cm[...], (((1,), (1,)), ((), ())), preferred_element_type=jnp.float32)
+    g = 1.0 / (TAU * 10.0 * live_ref[0:1, 0:1])
+
+    def block(n, acc):
+        at = pl.multiple_of(n * RB, RB)
+        rows = rows_ref[pl.ds(at, RB), :]
+        b = [jnp.broadcast_to(b_ref[v][None], (RB // 8, 8, KC)).reshape(RB, KC) for v in range(2)]
+        s = [s_all[pl.ds(pl.multiple_of(v * ROWS + at, RB), RB), :] for v in range(VIEWS)]
+        t = [jnp.exp2(x * (LOG2E / TAU)) for x in s]
+        q1 = (t[0] * rows[:, 0:1]) * (t[0] * b[0])
+        q2 = (t[1] * rows[:, 1:2]) * (t[1] * b[1])
+        q1_ref[pl.ds(at, RB), :] = q1
+        q2_ref[pl.ds(at, RB), :] = q2
+        small = (s[2] + s[3]) + (s[4] + s[5])
+        term = q2 * (s[0] + small) + q1 * (s[1] + small)
+        gq1 = q1 * g
+        gq2 = q2 * g
+        gqs = gq1 + gq2
+        for v in range(VIEWS):
+            w = rows[:, 2 + v:3 + v] * (g if v < 2 else 2.0 * g)
+            sub = (gq2, gq1)[v] if v < 2 else gqs
+            g_all[pl.ds(pl.multiple_of(v * ROWS + at, RB), RB), :] = (t[v] * w - sub).astype(jnp.bfloat16)
+        for r in range(RB // 8):
+            for k in range(KC // 128):
+                acc = acc + term[r * 8:(r + 1) * 8, k * 128:(k + 1) * 128]
+        return acc
+
+    loss_acc[...] = lax.fori_loop(0, ROWS // RB, block, loss_acc[...])
+    dz_acc[...] += lax.dot_general(g_all[...], cm[...], (((1,), (0,)), ((), ())), preferred_element_type=jnp.float32)
+    dc_ref[...] = lax.dot_general(g_all[...], zall[...], (((0,), (0,)), ((), ())), preferred_element_type=jnp.float32)
+
+    @pl.when(i == STEPS - 1)
+    def _():
+        dz1_ref[...] = dz_acc[0:ROWS]
+        dz2_ref[...] = dz_acc[ROWS:2 * ROWS]
+        for j in range(4):
+            dzs_ref[j] = dz_acc[(2 + j) * ROWS:(3 + j) * ROWS]
+        lse = jnp.sum(rows_ref[:, 8:9])
+        lane0 = ((lax.broadcasted_iota(jnp.int32, (8, 128), 0) == 0)
+                 & (lax.broadcasted_iota(jnp.int32, (8, 128), 1) == 0))
+        tail = NUM_K - (STEPS - 1) * KC
+        dc_ref[tail:tail + 8, :] = loss_acc[...] * (1.0 / TAU) - jnp.where(lane0, lse, 0.0)
+
+
+def run_grads(z_one, z_two, z_small, protos, b, rows, live):
+    def whole(*shape):
+        return pl.BlockSpec(shape, lambda i: (0,) * len(shape))
+
+    f32 = jnp.float32
+    return pl.pallas_call(
+        grads_kernel,
+        grid=(STEPS,),
+        out_shape=(jax.ShapeDtypeStruct((ROWS, NUM_K), f32), jax.ShapeDtypeStruct((ROWS, NUM_K), f32),
+                   jax.ShapeDtypeStruct((ROWS, 128), f32), jax.ShapeDtypeStruct((ROWS, 128), f32),
+                   jax.ShapeDtypeStruct((4, ROWS, 128), f32), jax.ShapeDtypeStruct((PAD_K, 128), f32)),
+        in_specs=[whole(ROWS, 128), whole(ROWS, 128), whole(4, ROWS, 128),
+                  pl.BlockSpec((KC, 128), lambda i: (i, 0)),
+                  pl.BlockSpec((2, 8, KC), lambda i: (0, 0, i)),
+                  whole(ROWS, 128), whole(8, 128)],
+        out_specs=(pl.BlockSpec((ROWS, KC), lambda i: (0, i)), pl.BlockSpec((ROWS, KC), lambda i: (0, i)),
+                   whole(ROWS, 128), whole(ROWS, 128), whole(4, ROWS, 128),
+                   pl.BlockSpec((KC, 128), lambda i: (i, 0))),
+        scratch_shapes=[
+            pltpu.VMEM((VIEWS * ROWS, 128), jnp.bfloat16),
+            pltpu.VMEM((KC, 128), jnp.bfloat16),
+            pltpu.VMEM((VIEWS * ROWS, KC), f32),
+            pltpu.VMEM((VIEWS * ROWS, KC), jnp.bfloat16),
+            pltpu.VMEM((VIEWS * ROWS, 128), f32),
+            pltpu.VMEM((8, 128), f32),
+        ],
+        name="grads",
+        compiler_params=pltpu.CompilerParams(dimension_semantics=("arbitrary",)),
+    )(z_one, z_two, z_small, protos, b, rows, live)
+
+
+HALF = PAD_K // 2
+THIRD = HALF // 3
+ORDERS = (("x", "yz"), ("y", "xz"), ("z", "xy"))
+
+
+def total_kernel(part_ref, out_ref, r0, acc, r1, mid, r2,
+                 s0, v0, s1, v1, s2, v2, s3, v3, s4, v4, s5, v5):
+    me = lax.axis_index("data")
+    core = lax.rem(me, 2)
+    mate = me + 1 - 2 * core
+    lines = [group_of(me, a) for a, _ in ORDERS]
+    planes = [group_of(me, p) for _, p in ORDERS]
+    devs = [mate]
+    for _, others in lines:
+        devs += [d for _, d in others]
+    for n, (_, others) in enumerate(planes):
+        axes = ORDERS[n][1]
+        devs += [d for (_, d), offs in zip(others, [o for o in itertools.product(range(4), repeat=2) if any(o)]) if all(offs)]
+    enter(devs)()
+    mine = pl.multiple_of(core * HALF, HALF)
+    theirs = pl.multiple_of((1 - core) * HALF, HALF)
+    pending = []
+
+    def send(src, dst, ssem, rsem, dev):
+        c = pltpu.make_async_remote_copy(src, dst, ssem, rsem, device_id=(dev,), device_id_type=MESH)
+        c.start()
+        pending.append(c)
+
+    def arrived(dst, ssem, rsem, dev):
+        pltpu.make_async_remote_copy(dst, dst, ssem, rsem, device_id=(dev,), device_id_type=MESH).wait_recv()
+
+    for j in range(3):
+        send(part_ref.at[pl.ds(theirs + j * THIRD, THIRD)], r0.at[j], s0.at[j], v0.at[j], mate)
+    for j in range(3):
+        arrived(r0.at[j], s0.at[j], v0.at[j], mate)
+        acc[j] = part_ref[pl.ds(mine + j * THIRD, THIRD), :] + r0[j]
+        own, others = lines[j]
+        for k, (slot, dev) in enumerate(others):
+            send(acc.at[j, pl.ds(pl.multiple_of(slot * 128, 128), 128)], r1.at[j, own], s1.at[j, k], v1.at[j, own], dev)
+        r1[j, own] = acc[j, pl.ds(pl.multiple_of(own * 128, 128), 128), :]
+    for j in range(3):
+        own, others = lines[j]
+        for k, (slot, dev) in enumerate(others):
+            arrived(r1.at[j, slot], s1.at[j, k], v1.at[j, slot], dev)
+        mid[j] = (r1[j, 0] + r1[j, 1]) + (r1[j, 2] + r1[j, 3])
+        own, others = planes[j]
+        for k, (slot, dev) in enumerate(others):
+            send(mid.at[j, pl.ds(pl.multiple_of(slot * 8, 8), 8)], r2.at[j, own], s2.at[j, k], v2.at[j, own], dev)
+        r2[j, own] = mid[j, pl.ds(pl.multiple_of(own * 8, 8), 8), :]
+    for j in range(3):
+        own_line = lines[j][0]
+        own, others = planes[j]
+        for k, (slot, dev) in enumerate(others):
+            arrived(r2.at[j, slot], s2.at[j, k], v2.at[j, slot], dev)
+        total = r2[j, 0]
+        for q in range(1, 16):
+            total = total + r2[j, q]
+        spot = pl.ds(pl.multiple_of(mine + j * THIRD + own_line * 128 + own * 8, 8), 8)
+        out_ref[spot, :] = total
+        for k, (slot, dev) in enumerate(others):
+            send(out_ref.at[spot], out_ref.at[spot], s3.at[j, k], v3.at[j, own], dev)
+    for j in range(3):
+        own_line, line = lines[j]
+        own, others = planes[j]
+        base = mine + j * THIRD + own_line * 128
+        for k, (slot, dev) in enumerate(others):
+            arrived(out_ref.at[pl.ds(pl.multiple_of(base + slot * 8, 8), 8)], s3.at[j, k], v3.at[j, slot], dev)
+        spot = pl.ds(pl.multiple_of(base, 128), 128)
+        for k, (slot, dev) in enumerate(line):
+            send(out_ref.at[spot], out_ref.at[spot], s4.at[j, k], v4.at[j, own_line], dev)
+        send(out_ref.at[spot], out_ref.at[spot], s5.at[j, 3], v5.at[j, own_line], mate)
+    for j in range(3):
+        own_line, line = lines[j]
+        for k, (slot, dev) in enumerate(line):
+            spot = pl.ds(pl.multiple_of(mine + j * THIRD + slot * 128, 128), 128)
+            arrived(out_ref.at[spot], s4.at[j, k], v4.at[j, slot], dev)
+            send(out_ref.at[spot], out_ref.at[spot], s5.at[j, k], v5.at[j, slot], mate)
+    for j in range(3):
+        for p in range(4):
+            spot = pl.ds(pl.multiple_of(theirs + j * THIRD + p * 128, 128), 128)
+            arrived(out_ref.at[spot], s5.at[j, 0], v5.at[j, p], mate)
+    for c in pending:
+        c.wait_send()
+
+
+def run_total(part):
+    vmem = pl.BlockSpec(memory_space=pltpu.VMEM)
+    dma = pltpu.SemaphoreType.DMA
+    f32 = jnp.float32
+    return pl.pallas_call(
+        total_kernel,
+        out_shape=jax.ShapeDtypeStruct((PAD_K, 128), f32),
+        in_specs=[vmem],
+        out_specs=vmem,
+        scratch_shapes=[
+            pltpu.VMEM((3, THIRD, 128), f32),
+            pltpu.VMEM((3, THIRD, 128), f32),
+            pltpu.VMEM((3, 4, 128, 128), f32),
+            pltpu.VMEM((3, 128, 128), f32),
+            pltpu.VMEM((3, 16, 8, 128), f32),
+            dma((3,)), dma((3,)), dma((3, 3)), dma((3, 4)), dma((3, 15)), dma((3, 16)),
+            dma((3, 15)), dma((3, 16)), dma((3, 3)), dma((3, 4)), dma((3, 4)), dma((3, 4)),
+        ],
+        name="total",
+        compiler_params=pltpu.CompilerParams(collective_id=1, has_side_effects=True),
+    )(part)
 
 
 def local_step(z_one, z_two, z_small, protos, live_mask):
-    live_col = live_mask.astype(jnp.float32)[:, None]
-    z_all = jnp.concatenate([z_one[None], z_two[None], z_small], axis=0)
-    bmat, rows, live = run_codes(z_all, protos, live_mask[None, :])
-    live_total = live[0, 0]
-    pair_count = 2 + 2 * z_small.shape[0]
-    grad_scale = 1.0 / (TAU * live_total * pair_count)
-    b = bmat.reshape(2, 1, PAD_K)[:, :, :NUM_K]
-    scores = jnp.einsum("vnd,kd->vnk", z_all, protos, preferred_element_type=jnp.float32)
-    q = jnp.exp(scores[:2] / EPS) * b * rows[:, :2].T[:, :, None]
-    logp = scores / TAU - rows[:, 2:8].T[:, :, None]
-    q_one, q_two = q[0], q[1]
-    q_sum = q_one + q_two
-    cross_sum = jnp.sum(q_two * logp[0]) + jnp.sum(q_one * logp[1]) + jnp.sum(q_sum[None] * logp[2:])
-    grad_one = ((live_col * jnp.exp(logp[0]) - q_two) * grad_scale).astype(jnp.bfloat16)
-    grad_two = ((live_col * jnp.exp(logp[1]) - q_one) * grad_scale).astype(jnp.bfloat16)
-    grad_small = ((2.0 * live_col[None] * jnp.exp(logp[2:]) - q_sum[None]) * grad_scale).astype(jnp.bfloat16)
-    grads = jnp.concatenate([grad_one[None], grad_two[None], grad_small], axis=0)
-    dz = jnp.einsum("jnk,kd->jnd", grads, protos, preferred_element_type=jnp.float32)
-    dc_part = jnp.einsum("jnk,jnd->kd", grads, z_all, preferred_element_type=jnp.float32)
-    d_protos = lax.psum(dc_part, "data")
-    loss_total = -lax.psum(cross_sum, "data") / (live_total * pair_count)
-    return q_one, q_two, loss_total, dz[0], dz[1], dz[2:], d_protos
+    b, rows, live = run_codes(z_one, z_two, z_small, protos, live_mask[None, :])
+    q_one, q_two, dz_one, dz_two, dz_small, part = run_grads(z_one, z_two, z_small, protos, b, rows, live)
+    total = run_total(part)
+    loss_total = -jnp.sum(total[NUM_K:NUM_K + 8]) / (live[0, 0] * 10.0)
+    return q_one, q_two, loss_total, dz_one, dz_two, dz_small, total[:NUM_K]
 
 
 def solution(mesh):

time: 264 us -> 128 us (0.48)
  waiting for transfers between devices: 65.2 us -> 0 us
  Pallas kernels: 48.2 us -> 113 us
  blocking collectives: 63.8 us -> 0 us
  other arithmetic: 26.3 us -> 1.29 us
  matrix products: 24.6 us -> 0 us
  between operations: 19.3 us -> 3.13 us
  local copies, waits for them, and re-layouts: 15.9 us -> 9.81 us
    psum x1 -> x0, waiting for transfers between devices: 65.2 us -> none  [local_step(): d_protos = lax.psum(dc_part, 'data')]
    pallas_call x1 -> x3, Pallas kernels: 48.2 us -> 113 us  [the longest x1 48.4 us: run_codes(): pl.pallas_call(codes_kernel, out_shape=(jax.ShapeDtypeStruct((2, 8, PAD_K...]
    psum x1 -> x0, blocking collectives: 63.8 us -> none  [local_step(): loss_total = -lax.psum(cross_sum, 'data') / (live_total * pair_count)]
    dot_general x3 -> x0, matrix products: 24.6 us -> none  [the longest x1 15.7 us: local_step(): jnp.einsum('vnd,kd->vnk', z_all, protos, preferred_element_type=jnp.float32)]
    convert_element_type x3 -> x0, other arithmetic: 10.9 us -> none  [the longest x1 5.81 us: local_step(): ((live_col * jnp.exp(logp[0]) - q_two) * grad_scale).astype(jnp.bfloat16)]
    reduce_sum x1, other arithmetic: 8.91 us -> 1.29 us  [local_step(): loss_total = -jnp.sum(total[NUM_K:NUM_K + 8]) / (live[0, 0] * 10.0)]
    mul x2 -> x0, other arithmetic: 4.76 us -> none  [the longest x1 4.07 us: local_step(): q = jnp.exp(scores[:2] / EPS) * b * rows[:, :2].T[:, :, None]]
    unnamed x17 -> x4, local copies, waits for them, and re-layouts: 10.3 us -> 6 us
  transfers between devices with their start and end apart: 1 -> 0, of which waited for: 1 -> 0; matrix products, arithmetic and copies ran while one was open for 6% -> 0% of each run, Pallas kernels for 0% -> 0%
where the time goes in v2:
time: 128 us
  Pallas kernels  113 us (88%)
  local copies, waits for them, and re-layouts  9.81 us (8%)
  between operations  3.13 us (2%)
  other arithmetic  1.29 us (1%)
    pallas_call x1, Pallas kernels, run_codes(): pl.pallas_call(codes_kernel, out_shape=(jax.ShapeDtypeStruct((2, 8, PAD_K...  48.4 us
    pallas_call x1, Pallas kernels, run_grads(): pl.pallas_call(grads_kernel, grid=(STEPS,), out_shape=(jax.ShapeDtypeStru...  32.6 us
    pallas_call x1, Pallas kernels, run_total(): pl.pallas_call(total_kernel, out_shape=jax.ShapeDtypeStruct((PAD_K, 128),...  32.3 us
    unnamed x4, local copies, waits for them, and re-layouts  6 us
    slice x1, local copies, waits for them, and re-layouts, local_step(): return (q_one, q_two, loss_total, dz_one, dz_two, dz_small, total[:NUM_K])  2.62 us

profile of v2, /device:TPU:1, one launch (start us, length us, event | category | flops | bytes accessed | tf_op | source)
XLA Modules:
  0.0 127.5 jit_solution(8005171677649571539)
XLA Ops:
  0.6 48.4 %codes.1 = (f32[2,8,3072]{2,1,0:T(8,128)}, f32[256,128]{1,0:T(8,128)}, f32[8,128]{1,0:T(8,128)}) custom-call(bf16[256,128]{1,0:T(8,128)(2,1)} %z1_ref.3, bf16[256,128]{1,0:T(8,128)(2,1)} %z2_ref.3, bf16[4,256,128]{2,1,0:T(8,128)(2,1)} %zs_ref.3, bf16[3000,128]{1,0:T(8,128)(2,1)} %c_ref.3, s32[1,256]{1,0:T(1,128)} %bitcast.2), custom_call_target="tpu_custom_call" | custom-call | tf_op jit(solution)/shard_map/codes/pallas_call | solution.py:217
  49.0 32.6 %grads.1 = (f32[256,3000]{1,0:T(8,128)}, f32[256,3000]{1,0:T(8,128)}, f32[256,128]{1,0:T(8,128)}, f32[256,128]{1,0:T(8,128)}, f32[4,256,128]{2,1,0:T(8,128)}, /*index=5*/f32[3072,128]{1,0:T(8,128)}) custom-call(bf16[256,128]{1,0:T(8,128)(2,1)} %z1_ref.3, bf16[256,128]{1,0:T(8,128)(2,1)} %z2_ref.3, bf16[4,256,128]{2,1,0:T(8,128)(2,1)} %zs_ref.3, ...), custom_call_target="tpu_custom_call" | custom-call | tf_op jit(solution)/shard_map/grads/pallas_call | solution.py:314
  81.6 32.3 %total.1 = f32[3072,128]{1,0:T(8,128)} custom-call(f32[3072,128]{1,0:T(8,128)} %get-tuple-element.21.part_ref), custom_call_target="tpu_custom_call" | custom-call | tf_op jit(solution)/shard_map/total/pallas_call | solution.py:429
  114.0 1.3 %slice_reduce_fusion = f32[]{:T(128)} fusion(f32[3072,128]{1,0:T(8,128)} %total.1), kind=kLoop, calls=%fused_computation | loop fusion | flops 1023 | bytes 4100 | tf_op jit(solution)/shard_map/reduce_sum | solution.py:452
  115.9 1.2 slice.10
  117.8 2.6 %slice.11 = f32[3000,128]{1,0:T(8,128)} slice(f32[3072,128]{1,0:T(8,128)} %total.1), slice={[0:3000], [0:128]} | slice | bytes 3072000 | tf_op jit(solution)/shard_map/slice | solution.py:453
  120.4 0.0 copy-start
  120.4 3.7 %copy.12 = f32[256,3000]{0,1:T(8,128)} copy(f32[256,3000]{1,0:T(8,128)} %get-tuple-element.25) | data formatting | bytes 6144000
  124.1 0.0 copy-done
  124.1 2.3 %copy.13 = f32[256,3000]{0,1:T(8,128)} copy(f32[256,3000]{1,0:T(8,128)S(1)} %copy-done) | data formatting | bytes 6144000
Async XLA Ops:
  120.4 3.7 %copy-start = (f32[256,3000]{1,0:T(8,128)S(1)}, f32[256,3000]{1,0:T(8,128)}, u32[]{:S(2)}) copy-start(f32[256,3000]{1,0:T(8,128)} %get-tuple-element.26) | copy-start | bytes 9216004

commit v3 on v2

--- a/solution.py
+++ b/solution.py
@@ -20,6 +20,7 @@
 CHUNK = 256
 TAIL = NUM_K - FULL * CHUNK
 VIEWS = 6
+UNIT = 512
 
 MESH = pl.DeviceIdType.MESH
 STRIDE = {"x": 2, "y": 8, "z": 32}
@@ -51,9 +52,10 @@
     return lambda: pl.semaphore_wait(bar, len(devs))
 
 
-def codes_kernel(z1_ref, z2_ref, zs_ref, c_ref, m_ref, b_ref, rows_ref, live_ref,
-                 z_ref, zx, mcol, e, colsum, dcol, drecv, slots_a, slots_b,
-                 zsend, zrecv, asend, arecv, bsend, brecv, fsend, frecv):
+def codes_kernel(z1_ref, z2_ref, zs_ref, c_ref, m_ref, b_ref, rows_ref, live_ref, mix_ref, *rest):
+    t_ref = rest[:VIEWS]
+    (z_ref, zx, mcol, e, colsum, b8, dcol, drecv, slots_a, slots_b,
+     zsend, zrecv, asend, arecv, bsend, brecv, fsend, frecv) = rest[VIEWS:]
     me = lax.axis_index("data")
     core = lax.rem(me, 2)
     mate = me + 1 - 2 * core
@@ -114,25 +116,32 @@
     flat = lax.broadcasted_iota(jnp.int32, (TILES, 128), 0) * 128 + lax.broadcasted_iota(jnp.int32, (TILES, 128), 1)
     count = jnp.sum(mcol[0] + mcol[1], axis=0, keepdims=True)
 
-    def lse_of(view):
+    mask = m_ref[...].astype(jnp.float32)
+
+    def softmax_of(view):
         z_view = z_ref[view] if view < 2 else zs_ref[view - 2]
 
-        def step(i, acc):
-            at = pl.multiple_of(i * CHUNK, CHUNK)
-            s = lax.dot_general(z_view, c_ref[pl.ds(at, CHUNK), :], (((1,), (1,)), ((), ())),
+        def piece(at, n):
+            s = lax.dot_general(c_ref[pl.ds(at, n), :], z_view, (((1,), (1,)), ((), ())),
                                 preferred_element_type=jnp.float32)
             t = jnp.exp2(s * (LOG2E / TAU))
-            return acc + t[:, :128] + t[:, 128:]
-
-        acc = lax.fori_loop(0, FULL, step, jnp.zeros((ROWS, 128), jnp.float32))
-        s = lax.dot_general(z_view, c_ref[FULL * CHUNK:NUM_K, :], (((1,), (1,)), ((), ())),
-                            preferred_element_type=jnp.float32)
-        t = jnp.exp2(s * (LOG2E / TAU))
-        total = jnp.sum(acc, axis=1, keepdims=True) + jnp.sum(t, axis=1, keepdims=True)
-        live = mcol[0][:, :1]
-        rows_ref[:, 2 + view:3 + view] = live / total
-        lse = jnp.log(total) * (live if view < 2 else 2.0 * live)
-        rows_ref[:, 8:9] = lse if view == 0 else rows_ref[:, 8:9] + lse
+            t_ref[view][pl.ds(at, n), :] = t
+            if view == 2:
+                mix_ref[1, pl.ds(at, n), :] = s
+            elif view == 0:
+                mix_ref[0, pl.ds(at, n), :] = mix_ref[1, pl.ds(at, n), :] + s
+            else:
+                mix_ref[1, pl.ds(at, n), :] += s
+            return jnp.sum(t.reshape(n // 8, 8, ROWS), axis=0)
+
+        acc = lax.fori_loop(0, NUM_K // UNIT, lambda i, acc: acc + piece(pl.multiple_of(i * UNIT, UNIT), UNIT),
+                            jnp.zeros((8, ROWS), jnp.float32))
+        acc = acc + piece(NUM_K // UNIT * UNIT, NUM_K % UNIT)
+        total = jnp.sum(acc, axis=0, keepdims=True)
+        share = mask if view < 2 else 2.0 * mask
+        rows_ref[2 + view:3 + view, :] = share / total
+        lse = jnp.log(total) * share
+        rows_ref[8:9, :] = lse if view == 2 else rows_ref[8:9, :] + lse
 
     def exchange(slots, send, recv, it, own, others, work):
         copies = []
@@ -158,21 +167,22 @@
             if it == 0 and t == TILES - 1:
                 row = jnp.where(lane == NUM_K % 128, count, row)
             slots_a[it, own_a, t:t + 1, :] = row
-        total, copies = exchange(slots_a, asend, arecv, it, own_a, others_a, functools.partial(lse_of, 2 * it))
+        total, copies = exchange(slots_a, asend, arecv, it, own_a, others_a, functools.partial(softmax_of, (2, 4, 0)[it]))
         pending += copies
         slots_b[it, own_b] = total
-        total, copies = exchange(slots_b, bsend, brecv, it, own_b, others_b, functools.partial(lse_of, 2 * it + 1))
+        total, copies = exchange(slots_b, bsend, brecv, it, own_b, others_b, functools.partial(softmax_of, (3, 5, 1)[it]))
         pending += copies
         if it == 0:
             live_ref[...] = jnp.broadcast_to(total[TILES - 1:TILES, NUM_K % 128:NUM_K % 128 + 1], (8, 128))
         inside = flat < NUM_K
         bmat = jnp.where(inside, 1.0 / (NUM_K * jnp.where(inside, total, 1.0)), 0.0)
-        for t in range(TILES):
-            b_ref[core, :, t * 128:(t + 1) * 128] = jnp.broadcast_to(bmat[t:t + 1, :], (8, 128))
         if it == ITERS - 1:
+            b_ref[core] = bmat
             give_b = pltpu.make_async_remote_copy(b_ref.at[core], b_ref.at[core], fsend.at[0], frecv.at[0],
                                                   device_id=(mate,), device_id_type=MESH)
             give_b.start()
+        for t in range(TILES):
+            b8[:, t * 128:(t + 1) * 128] = jnp.broadcast_to(bmat[t:t + 1, :], (8, 128))
         if it < ITERS - 1:
             colsum[...] = jnp.zeros_like(colsum)
 
@@ -181,7 +191,7 @@
             acc = jnp.zeros((128, 128), jnp.float32)
             for t in range(TILES):
                 acc += (e[pl.ds(r0, 128), t * 128:(t + 1) * 128].reshape(16, 8, 128)
-                        * b_ref[core, :, t * 128:(t + 1) * 128][None]).reshape(128, 128)
+                        * b8[:, t * 128:(t + 1) * 128][None]).reshape(128, 128)
             d = jnp.sum(acc, axis=1, keepdims=True)
             a = jnp.where(d > 0, 1.0 / jnp.where(d > 0, d, 1.0), 0.0)
             if it == ITERS - 1:
@@ -205,10 +215,10 @@
                                  device_id=(mate,), device_id_type=MESH).wait_recv()
     give_a.wait()
     first = core == 0
-    own_r = dcol[:ROWS, :1]
-    mate_r = drecv[:, :1]
-    rows_ref[:, 0:1] = jnp.where(first, own_r, mate_r)
-    rows_ref[:, 1:2] = jnp.where(first, mate_r, own_r)
+    own_r = jnp.concatenate([dcol[:128, :].T, dcol[128:ROWS, :].T], axis=1)[:1]
+    mate_r = jnp.concatenate([drecv[:128, :].T, drecv[128:, :].T], axis=1)[:1]
+    rows_ref[0:1, :] = jnp.where(first, own_r, mate_r)
+    rows_ref[1:2, :] = jnp.where(first, mate_r, own_r)
 
 
 def run_codes(z_one, z_two, z_small, protos, mask_row):
@@ -216,17 +226,20 @@
     dma = pltpu.SemaphoreType.DMA
     return pl.pallas_call(
         codes_kernel,
-        out_shape=(jax.ShapeDtypeStruct((2, 8, PAD_K), jnp.float32),
-                   jax.ShapeDtypeStruct((ROWS, 128), jnp.float32),
-                   jax.ShapeDtypeStruct((8, 128), jnp.float32)),
+        out_shape=(pltpu.VMEM((2, TILES, 128), jnp.float32),
+                   pltpu.VMEM((16, ROWS), jnp.float32),
+                   pltpu.VMEM((8, 128), jnp.float32),
+                   pltpu.VMEM((2, NUM_K, ROWS), jnp.float32),
+                   *[pltpu.VMEM((NUM_K, ROWS), jnp.float32)] * VIEWS),
         in_specs=[vmem] * 5,
-        out_specs=(vmem,) * 3,
+        out_specs=(vmem,) * (4 + VIEWS),
         scratch_shapes=[
             pltpu.VMEM((2, ROWS, 128), jnp.bfloat16),
             pltpu.VMEM((ROWS, 128), jnp.bfloat16),
             pltpu.VMEM((2, ROWS, 128), jnp.float32),
             pltpu.VMEM((2 * ROWS, PAD_K), jnp.float32),
             pltpu.VMEM((1, PAD_K), jnp.float32),
+            pltpu.VMEM((8, PAD_K), jnp.float32),
             pltpu.VMEM((2 * ROWS, 128), jnp.float32),
             pltpu.VMEM((ROWS, 128), jnp.float32),
             pltpu.VMEM((ITERS, 16, TILES, 128), jnp.float32),
@@ -237,19 +250,22 @@
             dma((2,)), dma((2,)),
         ],
         name="codes",
-        compiler_params=pltpu.CompilerParams(collective_id=0, has_side_effects=True),
+        compiler_params=pltpu.CompilerParams(collective_id=0, has_side_effects=True, vmem_limit_bytes=26 << 20),
     )(z_one, z_two, z_small, protos, mask_row)
 
 
-KC = 512
-STEPS = PAD_K // KC
-RB = 16
-
-
-def grads_kernel(z1_ref, z2_ref, zs_ref, c_ref, b_ref, rows_ref, live_ref,
-                 q1_ref, q2_ref, dz1_ref, dz2_ref, dzs_ref, dc_ref,
-                 zall, cm, s_all, g_all, dz_acc, loss_acc):
+KC = 1000
+STEPS = NUM_K // KC
+RB = 8
+UNROLL = 5
+
+
+def grads_kernel(z1_ref, z2_ref, zs_ref, c_ref, b_ref, rows_ref, live_ref, mix_ref, *rest):
+    t_ref = rest[:VIEWS]
+    (q1_ref, q2_ref, dz1_ref, dz2_ref, dzs_ref, dc_ref, loss_ref,
+     zall, g_all, dz_acc, loss_acc, rvec, bcol) = rest[VIEWS:]
     i = pl.program_id(0)
+    g = 1.0 / (TAU * 10.0 * live_ref[0:1, 0:1])
 
     @pl.when(i == 0)
     def _():
@@ -259,39 +275,36 @@
             zall[(2 + j) * ROWS:(3 + j) * ROWS] = zs_ref[j]
         dz_acc[...] = jnp.zeros_like(dz_acc)
         loss_acc[...] = jnp.zeros_like(loss_acc)
-
-    row_id = lax.broadcasted_iota(jnp.int32, (KC, 128), 0) + i * KC
-    cm[...] = jnp.where(row_id < NUM_K, c_ref[...].astype(jnp.float32), 0.0).astype(jnp.bfloat16)
-    s_all[...] = lax.dot_general(zall[...], cm[...], (((1,), (1,)), ((), ())), preferred_element_type=jnp.float32)
-    g = 1.0 / (TAU * 10.0 * live_ref[0:1, 0:1])
+        for v in range(2 + VIEWS):
+            rvec[v] = jnp.broadcast_to(rows_ref[v:v + 1, :] * (1.0 if v < 2 else g), (8, ROWS))
+        for v in range(2):
+            for t in range(TILES // 8):
+                bt = jnp.concatenate([b_ref[v, t * 8:(t + 1) * 8, :]] * 16, axis=0).T
+                for k in range(8):
+                    at = (t * 8 + k) * 128
+                    bcol[v, at:at + 128, :] = jnp.broadcast_to(bt[:, k:k + 1], (128, 128))
 
     def block(n, acc):
         at = pl.multiple_of(n * RB, RB)
-        rows = rows_ref[pl.ds(at, RB), :]
-        b = [jnp.broadcast_to(b_ref[v][None], (RB // 8, 8, KC)).reshape(RB, KC) for v in range(2)]
-        s = [s_all[pl.ds(pl.multiple_of(v * ROWS + at, RB), RB), :] for v in range(VIEWS)]
-        t = [jnp.exp2(x * (LOG2E / TAU)) for x in s]
-        q1 = (t[0] * rows[:, 0:1]) * (t[0] * b[0])
-        q2 = (t[1] * rows[:, 1:2]) * (t[1] * b[1])
+        src = pl.multiple_of(i * KC + n * RB, RB)
+        t = [t_ref[v][pl.ds(src, RB), :] for v in range(VIEWS)]
+        b = [jnp.concatenate([bcol[v, pl.ds(src, RB), :]] * 2, axis=1) for v in range(2)]
+        q1 = (t[0] * rvec[0]) * (t[0] * b[0])
+        q2 = (t[1] * rvec[1]) * (t[1] * b[1])
         q1_ref[pl.ds(at, RB), :] = q1
         q2_ref[pl.ds(at, RB), :] = q2
-        small = (s[2] + s[3]) + (s[4] + s[5])
-        term = q2 * (s[0] + small) + q1 * (s[1] + small)
+        term = q2 * mix_ref[0, pl.ds(src, RB), :] + q1 * mix_ref[1, pl.ds(src, RB), :]
         gq1 = q1 * g
         gq2 = q2 * g
         gqs = gq1 + gq2
         for v in range(VIEWS):
-            w = rows[:, 2 + v:3 + v] * (g if v < 2 else 2.0 * g)
             sub = (gq2, gq1)[v] if v < 2 else gqs
-            g_all[pl.ds(pl.multiple_of(v * ROWS + at, RB), RB), :] = (t[v] * w - sub).astype(jnp.bfloat16)
-        for r in range(RB // 8):
-            for k in range(KC // 128):
-                acc = acc + term[r * 8:(r + 1) * 8, k * 128:(k + 1) * 128]
-        return acc
-
-    loss_acc[...] = lax.fori_loop(0, ROWS // RB, block, loss_acc[...])
-    dz_acc[...] += lax.dot_general(g_all[...], cm[...], (((1,), (0,)), ((), ())), preferred_element_type=jnp.float32)
-    dc_ref[...] = lax.dot_general(g_all[...], zall[...], (((0,), (0,)), ((), ())), preferred_element_type=jnp.float32)
+            g_all[pl.ds(at, RB), v * ROWS:(v + 1) * ROWS] = (t[v] * rvec[2 + v] - sub).astype(jnp.bfloat16)
+        return acc + term[:, :128] + term[:, 128:]
+
+    loss_acc[...] = lax.fori_loop(0, KC // RB, block, loss_acc[...], unroll=UNROLL)
+    dz_acc[...] += lax.dot_general(g_all[...], c_ref[...], (((0,), (0,)), ((), ())), preferred_element_type=jnp.float32)
+    dc_ref[...] = lax.dot_general(g_all[...], zall[...], (((1,), (0,)), ((), ())), preferred_element_type=jnp.float32)
 
     @pl.when(i == STEPS - 1)
     def _():
@@ -299,42 +312,41 @@
         dz2_ref[...] = dz_acc[ROWS:2 * ROWS]
         for j in range(4):
             dzs_ref[j] = dz_acc[(2 + j) * ROWS:(3 + j) * ROWS]
-        lse = jnp.sum(rows_ref[:, 8:9])
+        lse = jnp.sum(rows_ref[8:9, :])
         lane0 = ((lax.broadcasted_iota(jnp.int32, (8, 128), 0) == 0)
                  & (lax.broadcasted_iota(jnp.int32, (8, 128), 1) == 0))
-        tail = NUM_K - (STEPS - 1) * KC
-        dc_ref[tail:tail + 8, :] = loss_acc[...] * (1.0 / TAU) - jnp.where(lane0, lse, 0.0)
-
-
-def run_grads(z_one, z_two, z_small, protos, b, rows, live):
+        loss_ref[...] = loss_acc[...] * (1.0 / TAU) - jnp.where(lane0, lse, 0.0)
+
+
+def run_grads(z_one, z_two, z_small, protos, b, rows, live, mix, t):
     def whole(*shape):
         return pl.BlockSpec(shape, lambda i: (0,) * len(shape))
 
     f32 = jnp.float32
+    vmem = pl.BlockSpec(memory_space=pltpu.VMEM)
     return pl.pallas_call(
         grads_kernel,
         grid=(STEPS,),
-        out_shape=(jax.ShapeDtypeStruct((ROWS, NUM_K), f32), jax.ShapeDtypeStruct((ROWS, NUM_K), f32),
+        out_shape=(jax.ShapeDtypeStruct((NUM_K, ROWS), f32), jax.ShapeDtypeStruct((NUM_K, ROWS), f32),
                    jax.ShapeDtypeStruct((ROWS, 128), f32), jax.ShapeDtypeStruct((ROWS, 128), f32),
-                   jax.ShapeDtypeStruct((4, ROWS, 128), f32), jax.ShapeDtypeStruct((PAD_K, 128), f32)),
+                   jax.ShapeDtypeStruct((4, ROWS, 128), f32), jax.ShapeDtypeStruct((NUM_K, 128), f32),
+                   jax.ShapeDtypeStruct((8, 128), f32)),
         in_specs=[whole(ROWS, 128), whole(ROWS, 128), whole(4, ROWS, 128),
-                  pl.BlockSpec((KC, 128), lambda i: (i, 0)),
-                  pl.BlockSpec((2, 8, KC), lambda i: (0, 0, i)),
-                  whole(ROWS, 128), whole(8, 128)],
-        out_specs=(pl.BlockSpec((ROWS, KC), lambda i: (0, i)), pl.BlockSpec((ROWS, KC), lambda i: (0, i)),
+                  pl.BlockSpec((KC, 128), lambda i: (i, 0)), vmem, vmem, vmem, vmem] + [vmem] * VIEWS,
+        out_specs=(pl.BlockSpec((KC, ROWS), lambda i: (i, 0)), pl.BlockSpec((KC, ROWS), lambda i: (i, 0)),
                    whole(ROWS, 128), whole(ROWS, 128), whole(4, ROWS, 128),
-                   pl.BlockSpec((KC, 128), lambda i: (i, 0))),
+                   pl.BlockSpec((KC, 128), lambda i: (i, 0)), whole(8, 128)),
         scratch_shapes=[
             pltpu.VMEM((VIEWS * ROWS, 128), jnp.bfloat16),
-            pltpu.VMEM((KC, 128), jnp.bfloat16),
-            pltpu.VMEM((VIEWS * ROWS, KC), f32),
-            pltpu.VMEM((VIEWS * ROWS, KC), jnp.bfloat16),
+            pltpu.VMEM((KC, VIEWS * ROWS), jnp.bfloat16),
             pltpu.VMEM((VIEWS * ROWS, 128), f32),
             pltpu.VMEM((8, 128), f32),
+            pltpu.VMEM((2 + VIEWS, 8, ROWS), f32),
+            pltpu.VMEM((2, PAD_K, 128), f32),
         ],
         name="grads",
-        compiler_params=pltpu.CompilerParams(dimension_semantics=("arbitrary",)),
-    )(z_one, z_two, z_small, protos, b, rows, live)
+        compiler_params=pltpu.CompilerParams(dimension_semantics=("arbitrary",), vmem_limit_bytes=26 << 20),
+    )(z_one, z_two, z_small, protos, b, rows, live, mix, *t)
 
 
 HALF = PAD_K // 2
@@ -342,7 +354,7 @@
 ORDERS = (("x", "yz"), ("y", "xz"), ("z", "xy"))
 
 
-def total_kernel(part_ref, out_ref, r0, acc, r1, mid, r2,
+def total_kernel(dc_ref, loss_ref, dout_ref, lout_ref, part_ref, out_ref, r0, acc, r1, mid, r2,
                  s0, v0, s1, v1, s2, v2, s3, v3, s4, v4, s5, v5):
     me = lax.axis_index("data")
     core = lax.rem(me, 2)
@@ -355,6 +367,9 @@
     for n, (_, others) in enumerate(planes):
         axes = ORDERS[n][1]
         devs += [d for (_, d), offs in zip(others, [o for o in itertools.product(range(4), repeat=2) if any(o)]) if all(offs)]
+    part_ref[:NUM_K, :] = dc_ref[...]
+    part_ref[NUM_K:NUM_K + 8, :] = loss_ref[...]
+    part_ref[NUM_K + 8:, :] = jnp.zeros((PAD_K - NUM_K - 8, 128), jnp.float32)
     enter(devs)()
     mine = pl.multiple_of(core * HALF, HALF)
     theirs = pl.multiple_of((1 - core) * HALF, HALF)
@@ -418,20 +433,24 @@
         for p in range(4):
             spot = pl.ds(pl.multiple_of(theirs + j * THIRD + p * 128, 128), 128)
             arrived(out_ref.at[spot], s5.at[j, 0], v5.at[j, p], mate)
+    dout_ref[...] = out_ref[:NUM_K, :]
+    lout_ref[...] = out_ref[NUM_K:NUM_K + 8, :]
     for c in pending:
         c.wait_send()
 
 
-def run_total(part):
+def run_total(part, loss):
     vmem = pl.BlockSpec(memory_space=pltpu.VMEM)
     dma = pltpu.SemaphoreType.DMA
     f32 = jnp.float32
     return pl.pallas_call(
         total_kernel,
-        out_shape=jax.ShapeDtypeStruct((PAD_K, 128), f32),
-        in_specs=[vmem],
-        out_specs=vmem,
+        out_shape=(jax.ShapeDtypeStruct((NUM_K, 128), f32), jax.ShapeDtypeStruct((8, 128), f32)),
+        in_specs=[vmem, vmem],
+        out_specs=(vmem, vmem),
         scratch_shapes=[
+            pltpu.VMEM((PAD_K, 128), f32),
+            pltpu.VMEM((PAD_K, 128), f32),
             pltpu.VMEM((3, THIRD, 128), f32),
             pltpu.VMEM((3, THIRD, 128), f32),
             pltpu.VMEM((3, 4, 128, 128), f32),
@@ -441,16 +460,17 @@
             dma((3, 15)), dma((3, 16)), dma((3, 3)), dma((3, 4)), dma((3, 4)), dma((3, 4)),
         ],
         name="total",
-        compiler_params=pltpu.CompilerParams(collective_id=1, has_side_effects=True),
-    )(part)
+        compiler_params=pltpu.CompilerParams(collective_id=1, has_side_effects=True, vmem_limit_bytes=16 << 20),
+    )(part, loss)
 
 
 def local_step(z_one, z_two, z_small, protos, live_mask):
-    b, rows, live = run_codes(z_one, z_two, z_small, protos, live_mask[None, :])
-    q_one, q_two, dz_one, dz_two, dz_small, part = run_grads(z_one, z_two, z_small, protos, b, rows, live)
-    total = run_total(part)
-    loss_total = -jnp.sum(total[NUM_K:NUM_K + 8]) / (live[0, 0] * 10.0)
-    return q_one, q_two, loss_total, dz_one, dz_two, dz_small, total[:NUM_K]
+    b, rows, live, mix, *t = run_codes(z_one, z_two, z_small, protos, live_mask[None, :])
+    q_one, q_two, dz_one, dz_two, dz_small, part, loss = run_grads(
+        z_one, z_two, z_small, protos, b, rows, live, mix, t)
+    total, loss_sum = run_total(part, loss)
+    loss_total = -jnp.sum(loss_sum) / (live[0, 0] * 10.0)
+    return q_one.T, q_two.T, loss_total, dz_one, dz_two, dz_small, total
 
 
 def solution(mesh):

time: 128 us -> 99.2 us (0.78)
  Pallas kernels: 113 us -> 89.1 us
  local copies, waits for them, and re-layouts: 9.81 us -> 6.07 us
    pallas_call x1, Pallas kernels: 32.6 us -> 12.7 us  [run_grads(): pl.pallas_call(grads_kernel, grid=(STEPS,), out_shape=(jax.ShapeDtypeStru...]
    pallas_call x2, Pallas kernels: 80.7 us -> 76.4 us  [the longest x1 46.3 us: run_codes(): pl.pallas_call(codes_kernel, out_shape=(pltpu.VMEM((2, TILES, 128), jnp.f...]
    slice x2 -> x1, local copies, waits for them, and re-layouts: 3.81 us -> 0.51 us  [local_step(): loss_total = -jnp.sum(loss_sum) / (live[0, 0] * 10.0)]
    unnamed x4 -> x11, local copies, waits for them, and re-layouts: 6 us -> 5.56 us
where the time goes in v3:
time: 99.2 us; the launch traced here: 98.9 us
  Pallas kernels  89.1 us (90%)
  local copies, waits for them, and re-layouts  6.07 us (6%)
  between operations  3.14 us (3%)
    pallas_call x1, Pallas kernels, run_codes(): pl.pallas_call(codes_kernel, out_shape=(pltpu.VMEM((2, TILES, 128), jnp.f...  46.3 us
    pallas_call x1, Pallas kernels, run_total(): pl.pallas_call(total_kernel, out_shape=(jax.ShapeDtypeStruct((NUM_K, 128)...  30.1 us
    pallas_call x1, Pallas kernels, run_grads(): pl.pallas_call(grads_kernel, grid=(STEPS,), out_shape=(jax.ShapeDtypeStru...  12.7 us
    unnamed x11, local copies, waits for them, and re-layouts  5.56 us

profile of v3, /device:TPU:1, one launch (start us, length us, event | category | flops | bytes accessed | tf_op | source)
XLA Modules:
  0.0 98.9 jit_solution(1913480220309026673)
XLA Ops:
  0.6 0.0 copy-start
  0.6 1.1 %copy-done = bf16[3000,128]{1,0:T(8,128)(2,1)S(1)} copy-done((bf16[3000,128]{1,0:T(8,128)(2,1)S(1)}, bf16[3000,128]{1,0:T(8,128)(2,1)}, u32[]{:S(2)}) %copy-start) | copy-done | bytes 768024
  1.8 0.0 copy-start.1
  1.8 0.9 copy-done.1
  2.7 0.0 copy-start.2
  2.7 0.8 copy-done.2
  3.6 0.0 copy-start.3
  3.6 0.8 copy-done.3
  4.4 0.0 copy-start.4
  4.4 0.7 copy-done.4
  5.1 46.3 %codes.1 = (f32[2,24,128]{2,1,0:T(8,128)S(1)}, f32[16,256]{1,0:T(8,128)S(1)}, f32[8,128]{1,0:T(8,128)S(1)}, f32[2,3000,256]{2,1,0:T(8,128)S(1)}, f32[3000,256]{1...) custom-call(bf16[256,128]{1,0:T(8,128)(2,1)S(1)} %copy-done.2, ...), custom_call_target="tpu_custom_call" | custom-call | tf_op jit(solution)/shard_map/codes/pallas_call | solution.py:227
  51.4 12.7 %grads.1 = (f32[3000,256]{1,0:T(8,128)}, f32[3000,256]{1,0:T(8,128)}, f32[256,128]{1,0:T(8,128)}, f32[256,128]{1,0:T(8,128)}, f32[4,256,128]{2,1,0:T(8,128)}, /*...) custom-call(bf16[256,128]{1,0:T(8,128)(2,1)S(1)} %copy-done.2, bf16[256,128]{1,0:T(8,128)(2,1)S(1)} %copy-done.3, ...), custom_call_target="tpu_custom_call" | custom-call | tf_op jit(solution)/shard_map/grads/pallas_call | solution.py:327
  64.1 30.1 %total.1 = (f32[3000,128]{1,0:T(8,128)S(1)}, f32[8,128]{1,0:T(8,128)S(1)}) custom-call(f32[3000,128]{1,0:T(8,128)S(1)} %get-tuple-element.38.dc_ref, f32[8,128]{1,0:T(8,128)S(1)} %get-tuple-element.39.loss_ref), custom_call_target="tpu_custom_call" | custom-call | tf_op jit(solution)/shard_map/total/pallas_call | solution.py:446
  94.2 0.6 reduce_sum.9
  95.4 0.5 slice.3
  96.6 1.1 %copy.13 = f32[3000,128]{1,0:T(8,128)} copy(f32[3000,128]{1,0:T(8,128)S(1)} %get-tuple-element.58) | data formatting | bytes 3072000
Async XLA Ops:
  0.6 1.1 %copy-start = (bf16[3000,128]{1,0:T(8,128)(2,1)S(1)}, bf16[3000,128]{1,0:T(8,128)(2,1)}, u32[]{:S(2)}) copy-start(bf16[3000,128]{1,0:T(8,128)(2,1)} %c_ref.3) | copy-start | bytes 2304004
  1.8 0.9 copy-start.1
  2.7 0.8 copy-start.2
  3.6 0.8 copy-start.3
  4.4 0.7 copy-start.4

commit v4 on v3

--- a/solution.py
+++ b/solution.py
@@ -16,8 +16,8 @@
 NUM_K = 3000
 PAD_K = 3072
 TILES = PAD_K // 128
-FULL = 11
-CHUNK = 256
+CHUNK = 512
+FULL = NUM_K // CHUNK
 TAIL = NUM_K - FULL * CHUNK
 VIEWS = 6
 UNIT = 512
@@ -52,9 +52,9 @@
     return lambda: pl.semaphore_wait(bar, len(devs))
 
 
-def codes_kernel(z1_ref, z2_ref, zs_ref, c_ref, m_ref, b_ref, rows_ref, live_ref, mix_ref, *rest):
+def codes_kernel(z1_hbm, z2_hbm, zs_hbm, c_hbm, m_hbm, b_ref, rows_ref, live_ref, z_ref, c_ref, mix_ref, *rest):
     t_ref = rest[:VIEWS]
-    (z_ref, zx, mcol, e, colsum, b8, dcol, drecv, slots_a, slots_b,
+    (m_ref, insem, zx, mcol, e, colsum, b8, dcol, drecv, slots_a, slots_b,
      zsend, zrecv, asend, arecv, bsend, brecv, fsend, frecv) = rest[VIEWS:]
     me = lax.axis_index("data")
     core = lax.rem(me, 2)
@@ -63,8 +63,15 @@
     own_b, others_b = group_of(me, "z")
     entered = enter([mate] + [d for _, d in others_a] + [d for _, d in others_b])
 
-    z_ref[0] = z1_ref[...]
-    z_ref[1] = z2_ref[...]
+    loads = [pltpu.make_async_copy(m_hbm, m_ref, insem.at[0]),
+             pltpu.make_async_copy(z1_hbm, z_ref.at[0], insem.at[1]),
+             pltpu.make_async_copy(z2_hbm, z_ref.at[1], insem.at[2]),
+             pltpu.make_async_copy(c_hbm, c_ref, insem.at[3]),
+             pltpu.make_async_copy(zs_hbm, z_ref.at[pl.ds(2, 4)], insem.at[4])]
+    for c in loads:
+        c.start()
+    for c in loads:
+        c.wait()
     mrow = jnp.broadcast_to(m_ref[...].astype(jnp.float32), (128, ROWS))
     mcol[0] = jnp.concatenate([mrow[:, :128].T, mrow[:, 128:].T], axis=0)
 
@@ -91,13 +98,13 @@
         s = lax.dot_general(z_half, c_ref[FULL * CHUNK:NUM_K, :], (((1,), (1,)), ((), ())),
                             preferred_element_type=jnp.float32)
         v = piece(s)
-        e[half * ROWS:(half + 1) * ROWS, FULL * CHUNK + 128:] = jnp.zeros((ROWS, 128), jnp.float32)
+        e[half * ROWS:(half + 1) * ROWS, NUM_K // 128 * 128:] = jnp.zeros((ROWS, 128), jnp.float32)
         e[half * ROWS:(half + 1) * ROWS, FULL * CHUNK:NUM_K] = v
         part = jnp.sum(v, axis=0, keepdims=True)
         if half:
             colsum[:, FULL * CHUNK:NUM_K] += part
         else:
-            colsum[:, FULL * CHUNK + 128:] = jnp.zeros((1, 128), jnp.float32)
+            colsum[:, NUM_K // 128 * 128:] = jnp.zeros((1, 128), jnp.float32)
             colsum[:, FULL * CHUNK:NUM_K] = part
 
     entered()
@@ -119,7 +126,7 @@
     mask = m_ref[...].astype(jnp.float32)
 
     def softmax_of(view):
-        z_view = z_ref[view] if view < 2 else zs_ref[view - 2]
+        z_view = z_ref[view]
 
         def piece(at, n):
             s = lax.dot_general(c_ref[pl.ds(at, n), :], z_view, (((1,), (1,)), ((), ())),
@@ -222,6 +229,7 @@
 
 
 def run_codes(z_one, z_two, z_small, protos, mask_row):
+    hbm = pl.BlockSpec(memory_space=pltpu.HBM)
     vmem = pl.BlockSpec(memory_space=pltpu.VMEM)
     dma = pltpu.SemaphoreType.DMA
     return pl.pallas_call(
@@ -229,12 +237,15 @@
         out_shape=(pltpu.VMEM((2, TILES, 128), jnp.float32),
                    pltpu.VMEM((16, ROWS), jnp.float32),
                    pltpu.VMEM((8, 128), jnp.float32),
+                   pltpu.VMEM((VIEWS, ROWS, 128), jnp.bfloat16),
+                   pltpu.VMEM((NUM_K, 128), jnp.bfloat16),
                    pltpu.VMEM((2, NUM_K, ROWS), jnp.float32),
                    *[pltpu.VMEM((NUM_K, ROWS), jnp.float32)] * VIEWS),
-        in_specs=[vmem] * 5,
-        out_specs=(vmem,) * (4 + VIEWS),
+        in_specs=[hbm] * 5,
+        out_specs=(vmem,) * (6 + VIEWS),
         scratch_shapes=[
-            pltpu.VMEM((2, ROWS, 128), jnp.bfloat16),
+            pltpu.VMEM((1, ROWS), jnp.int32),
+            dma((5,)),
             pltpu.VMEM((ROWS, 128), jnp.bfloat16),
             pltpu.VMEM((2, ROWS, 128), jnp.float32),
             pltpu.VMEM((2 * ROWS, PAD_K), jnp.float32),
@@ -251,7 +262,7 @@
         ],
         name="codes",
         compiler_params=pltpu.CompilerParams(collective_id=0, has_side_effects=True, vmem_limit_bytes=26 << 20),
-    )(z_one, z_two, z_small, protos, mask_row)
+    )(*[pltpu.with_memory_space_constraint(x, pltpu.HBM) for x in (z_one, z_two, z_small, protos, mask_row)])
 
 
 KC = 1000
@@ -260,19 +271,15 @@
 UNROLL = 5
 
 
-def grads_kernel(z1_ref, z2_ref, zs_ref, c_ref, b_ref, rows_ref, live_ref, mix_ref, *rest):
+def grads_kernel(z_ref, c_ref, b_ref, rows_ref, live_ref, mix_ref, *rest):
     t_ref = rest[:VIEWS]
     (q1_ref, q2_ref, dz1_ref, dz2_ref, dzs_ref, dc_ref, loss_ref,
-     zall, g_all, dz_acc, loss_acc, rvec, bcol) = rest[VIEWS:]
+     g_all, dz_acc, loss_acc, rvec, bcol) = rest[VIEWS:]
     i = pl.program_id(0)
     g = 1.0 / (TAU * 10.0 * live_ref[0:1, 0:1])
 
     @pl.when(i == 0)
     def _():
-        zall[0:ROWS] = z1_ref[...]
-        zall[ROWS:2 * ROWS] = z2_ref[...]
-        for j in range(4):
-            zall[(2 + j) * ROWS:(3 + j) * ROWS] = zs_ref[j]
         dz_acc[...] = jnp.zeros_like(dz_acc)
         loss_acc[...] = jnp.zeros_like(loss_acc)
         for v in range(2 + VIEWS):
@@ -303,8 +310,10 @@
         return acc + term[:, :128] + term[:, 128:]
 
     loss_acc[...] = lax.fori_loop(0, KC // RB, block, loss_acc[...], unroll=UNROLL)
-    dz_acc[...] += lax.dot_general(g_all[...], c_ref[...], (((0,), (0,)), ((), ())), preferred_element_type=jnp.float32)
-    dc_ref[...] = lax.dot_general(g_all[...], zall[...], (((1,), (0,)), ((), ())), preferred_element_type=jnp.float32)
+    zall = z_ref[...].reshape(VIEWS * ROWS, 128)
+    c_part = c_ref[pl.ds(pl.multiple_of(i * KC, 8), KC), :]
+    dz_acc[...] += lax.dot_general(g_all[...], c_part, (((0,), (0,)), ((), ())), preferred_element_type=jnp.float32)
+    dc_ref[...] = lax.dot_general(g_all[...], zall, (((1,), (0,)), ((), ())), preferred_element_type=jnp.float32)
 
     @pl.when(i == STEPS - 1)
     def _():
@@ -318,7 +327,7 @@
         loss_ref[...] = loss_acc[...] * (1.0 / TAU) - jnp.where(lane0, lse, 0.0)
 
 
-def run_grads(z_one, z_two, z_small, protos, b, rows, live, mix, t):
+def run_grads(z, c, b, rows, live, mix, t):
     def whole(*shape):
         return pl.BlockSpec(shape, lambda i: (0,) * len(shape))
 
@@ -331,13 +340,11 @@
                    jax.ShapeDtypeStruct((ROWS, 128), f32), jax.ShapeDtypeStruct((ROWS, 128), f32),
                    jax.ShapeDtypeStruct((4, ROWS, 128), f32), jax.ShapeDtypeStruct((NUM_K, 128), f32),
                    jax.ShapeDtypeStruct((8, 128), f32)),
-        in_specs=[whole(ROWS, 128), whole(ROWS, 128), whole(4, ROWS, 128),
-                  pl.BlockSpec((KC, 128), lambda i: (i, 0)), vmem, vmem, vmem, vmem] + [vmem] * VIEWS,
+        in_specs=[vmem] * (6 + VIEWS),
         out_specs=(pl.BlockSpec((KC, ROWS), lambda i: (i, 0)), pl.BlockSpec((KC, ROWS), lambda i: (i, 0)),
                    whole(ROWS, 128), whole(ROWS, 128), whole(4, ROWS, 128),
                    pl.BlockSpec((KC, 128), lambda i: (i, 0)), whole(8, 128)),
         scratch_shapes=[
-            pltpu.VMEM((VIEWS * ROWS, 128), jnp.bfloat16),
             pltpu.VMEM((KC, VIEWS * ROWS), jnp.bfloat16),
             pltpu.VMEM((VIEWS * ROWS, 128), f32),
             pltpu.VMEM((8, 128), f32),
@@ -346,7 +353,7 @@
         ],
         name="grads",
         compiler_params=pltpu.CompilerParams(dimension_semantics=("arbitrary",), vmem_limit_bytes=26 << 20),
-    )(z_one, z_two, z_small, protos, b, rows, live, mix, *t)
+    )(z, c, b, rows, live, mix, *t)
 
 
 HALF = PAD_K // 2
@@ -464,13 +471,33 @@
     )(part, loss)
 
 
+def finish_kernel(dc_ref, sum_ref, live_ref, out_ref, loss_ref, sem):
+    copy = pltpu.make_async_copy(dc_ref, out_ref, sem)
+    copy.start()
+    total = jnp.sum(jnp.sum(sum_ref[...], axis=0, keepdims=True), axis=1, keepdims=True)
+    loss_ref[...] = -total / (live_ref[0:1, 0:1] * 10.0)
+    copy.wait()
+
+
+def run_finish(total, loss_sum, live):
+    vmem = pl.BlockSpec(memory_space=pltpu.VMEM)
+    return pl.pallas_call(
+        finish_kernel,
+        out_shape=(jax.ShapeDtypeStruct((NUM_K, 128), jnp.float32), jax.ShapeDtypeStruct((1, 1), jnp.float32)),
+        in_specs=[vmem] * 3,
+        out_specs=(pl.BlockSpec(memory_space=pltpu.HBM), vmem),
+        scratch_shapes=[pltpu.SemaphoreType.DMA],
+        name="finish",
+        compiler_params=pltpu.CompilerParams(vmem_limit_bytes=8 << 20),
+    )(total, loss_sum, live)
+
+
 def local_step(z_one, z_two, z_small, protos, live_mask):
-    b, rows, live, mix, *t = run_codes(z_one, z_two, z_small, protos, live_mask[None, :])
-    q_one, q_two, dz_one, dz_two, dz_small, part, loss = run_grads(
-        z_one, z_two, z_small, protos, b, rows, live, mix, t)
+    b, rows, live, z, c, mix, *t = run_codes(z_one, z_two, z_small, protos, live_mask[None, :])
+    q_one, q_two, dz_one, dz_two, dz_small, part, loss = run_grads(z, c, b, rows, live, mix, t)
     total, loss_sum = run_total(part, loss)
-    loss_total = -jnp.sum(loss_sum) / (live[0, 0] * 10.0)
-    return q_one.T, q_two.T, loss_total, dz_one, dz_two, dz_small, total
+    d_protos, loss_total = run_finish(total, loss_sum, live)
+    return q_one.T, q_two.T, loss_total.reshape(()), dz_one, dz_two, dz_small, d_protos
 
 
 def solution(mesh):

time: 99.2 us -> 89.7 us (0.904)
  local copies, waits for them, and re-layouts: 6.07 us -> 0 us
  between operations: 3.14 us -> 0.65 us
    unnamed x11 -> x0, local copies, waits for them, and re-layouts: 5.56 us -> none
    pallas_call x1, Pallas kernels: 46.3 us -> 44.3 us  [run_codes(): pl.pallas_call(codes_kernel, out_shape=(pltpu.VMEM((2, TILES, 128), jnp.f...]
    pallas_call x0 -> x1, Pallas kernels: none -> 1.65 us  [run_finish(): pl.pallas_call(finish_kernel, out_shape=(jax.ShapeDtypeStruct((NUM_K, 128...]
where the time goes in v4:
time: 89.7 us; the launch traced here: 89.5 us
  Pallas kernels  88.9 us (99%)
    pallas_call x1, Pallas kernels, run_codes(): pl.pallas_call(codes_kernel, out_shape=(pltpu.VMEM((2, TILES, 128), jnp.f...  44.3 us
    pallas_call x1, Pallas kernels, run_total(): pl.pallas_call(total_kernel, out_shape=(jax.ShapeDtypeStruct((NUM_K, 128)...  30.1 us
    pallas_call x1, Pallas kernels, run_grads(): pl.pallas_call(grads_kernel, grid=(STEPS,), out_shape=(jax.ShapeDtypeStru...  12.8 us

profile of v4, /device:TPU:1, one launch (start us, length us, event | category | flops | bytes accessed | tf_op | source)
XLA Modules:
  0.0 89.5 jit_solution(14974931435664915300)
XLA Ops:
  0.6 44.3 %codes.1 = (f32[2,24,128]{2,1,0:T(8,128)S(1)}, f32[16,256]{1,0:T(8,128)S(1)}, f32[8,128]{1,0:T(8,128)S(1)}, bf16[6,256,128]{2,1,0:T(8,128)(2,1)S(1)}, bf16[3000,...) custom-call(bf16[256,128]{1,0:T(8,128)(2,1)} %z1_hbm.1, ...), custom_call_target="tpu_custom_call" | custom-call | tf_op jit(solution)/shard_map/codes/pallas_call | solution.py:235
  45.0 12.8 %grads.1 = (f32[3000,256]{1,0:T(8,128)}, f32[3000,256]{1,0:T(8,128)}, f32[256,128]{1,0:T(8,128)}, f32[256,128]{1,0:T(8,128)}, f32[4,256,128]{2,1,0:T(8,128)}, /*...) custom-call(bf16[6,256,128]{2,1,0:T(8,128)(2,1)S(1)} %get-tuple-element.30.z_ref, ...), custom_call_target="tpu_custom_call" | custom-call | tf_op jit(solution)/shard_map/grads/pallas_call | solution.py:336
  57.8 30.1 %total.1 = (f32[3000,128]{1,0:T(8,128)S(1)}, f32[8,128]{1,0:T(8,128)S(1)}) custom-call(f32[3000,128]{1,0:T(8,128)S(1)} %get-tuple-element.44.dc_ref, f32[8,128]{1,0:T(8,128)S(1)} %get-tuple-element.45.loss_ref), custom_call_target="tpu_custom_call" | custom-call | tf_op jit(solution)/shard_map/total/pallas_call | solution.py:453
  87.9 1.7 %finish.1 = (f32[3000,128]{1,0:T(8,128)}, f32[1,1]{1,0:T(1,128)}) custom-call(f32[3000,128]{1,0:T(8,128)S(1)} %get-tuple-element.46.dc_ref, f32[8,128]{1,0:T(8,128)S(1)} %get-tuple-element.47.sum_ref, f32[8,128]{1,0:T(8,128)S(1)} %get-tuple-element.34.live_ref), custom_call_target="tpu_custom_call" | custom-call | tf_op jit(solution)/shard_map/finish/pallas_call | solution.py:484
